TPU v7x, 32 devices: a whole 2x2x4 slice. The times are simulated.
32 devices in a mesh: ma: 4 (over y, x), freq: 8 (over z, core).
Axes of the slice: x: 2, y: 2, z: 4, core: 2. Of those that a mesh axis runs over, the one named last changes fastest.
Arguments:
- m_table: int32 [8], P('ma'), may hold values from 0 to 1023, as said below
- retained_modes: int32 [8], P('ma'), may hold values from 128 to 512, as said below
- cycle_ids: int32 [32], P('ma'), may hold values from 1 to 2047, as said below
- kl_coeffs: bfloat16 [8, 4, 512], P('ma', None, 'freq'), may hold values from -6 to 6
- kl_vectors: bfloat16 [8, 512, 32, 512], P('ma', 'freq'), may hold values from -0.375 to 0.375
- beam_matrix: bfloat16 [8, 32, 1024, 512], P('ma', 'freq'), may hold values from -0.00390625 to 0.00390625
Outputs:
- sky_maps: float32 [32, 2, 32, 2048], P('ma', None, 'freq')
Inputs may be any that keep to these rules, and one draw needn't show every extreme that they name: `m_table`: all distinct; slots 2 q and 2 q + 1 hold two numbers that sum to 1023. `retained_modes`: some slot keeps all 512 modes. `cycle_ids`: all distinct.
All inputs are finite; a program needn't handle non-finite values.
Results may differ from a plain program's by a relative error of at most 0.01.
Values may be sent and summed in bfloat16 or wider, within the bound.
No kernel may reach another device: no remote copies, remote signals or barrier semaphores. Data moves between devices by JAX's collectives and lax.ppermute only.
A program may use at most 64 MiB of HBM per device.

v0:
```python
import math

import jax
import jax.numpy as jnp
from jax import lax
from jax.sharding import PartitionSpec as P

NPHI = 2048
L = 1024
NSIDE = 512


def cycle_angles(cycle_numbers):
    cycle_float = cycle_numbers.astype(jnp.float32)
    nside_float = float(NSIDE)
    from_pole = jnp.minimum(cycle_float, 4.0 * nside_float - cycle_float)
    hemisphere = jnp.where(cycle_float <= 2.0 * nside_float, 1.0, -1.0)
    polar_part = from_pole * from_pole / (3.0 * nside_float * nside_float)
    colatitude_cosine = 1.0 - polar_part
    polar_sin = from_pole / (math.sqrt(3.0) * nside_float) * jnp.sqrt(2.0 - polar_part)
    latitude_cosine = 4.0 / 3.0 - 2.0 * from_pole / (3.0 * nside_float)
    latitude_sine = jnp.sqrt(jnp.maximum(1.0 - latitude_cosine * latitude_cosine, 0.25))
    in_cap = from_pole < nside_float
    cos_theta = hemisphere * jnp.where(in_cap, colatitude_cosine, latitude_cosine)
    sin_theta = jnp.where(in_cap, polar_sin, latitude_sine)
    return (cos_theta, sin_theta)


def combine(before_part, after_part):
    upper_left = after_part[0] * before_part[0] + after_part[1] * before_part[2]
    upper_right = after_part[0] * before_part[1] + after_part[1] * before_part[3]
    lower_left = after_part[2] * before_part[0] + after_part[3] * before_part[2]
    lower_right = after_part[2] * before_part[1] + after_part[3] * before_part[3]
    weight = jnp.abs(upper_left) + jnp.abs(upper_right) + jnp.abs(lower_left) + jnp.abs(lower_right)
    return (
        upper_left / weight,
        upper_right / weight,
        lower_left / weight,
        lower_right / weight,
        before_part[4] + after_part[4] + jnp.log(weight),
    )


def legendre_rows(m_value, cos_theta, sin_theta):
    m_float = m_value.astype(jnp.float32)
    offset_rows = jnp.arange(L, dtype=jnp.float32)[:, None]
    later_rows = jnp.maximum(offset_rows, 2.0)
    degree = m_float + later_rows
    factor = jnp.sqrt((4.0 * degree * degree - 1.0) / (later_rows * (degree + m_float)))
    damping = jnp.sqrt(
        (later_rows - 1.0)
        * (degree - 1.0 + m_float)
        / (4.0 * (degree - 1.0) * (degree - 1.0) - 1.0)
    )
    first_step = jnp.sqrt(2.0 * m_float + 3.0)
    grid_shape = (L, cos_theta.shape[0])
    upper_left = jnp.where(
        offset_rows >= 2.0,
        factor * cos_theta[None, :],
        jnp.where(offset_rows >= 1.0, first_step * cos_theta[None, :], 1.0),
    )
    upper_right = jnp.broadcast_to(
        jnp.where(offset_rows >= 2.0, -factor * damping, 0.0), grid_shape
    )
    lower_left = jnp.broadcast_to(jnp.where(offset_rows >= 1.0, 1.0, 0.0), grid_shape)
    lower_right = jnp.broadcast_to(jnp.where(offset_rows >= 1.0, 0.0, 1.0), grid_shape)
    weight = jnp.abs(upper_left) + jnp.abs(upper_right) + jnp.abs(lower_left) + jnp.abs(lower_right)
    elements = (
        upper_left / weight,
        upper_right / weight,
        lower_left / weight,
        lower_right / weight,
        jnp.log(weight),
    )
    prefix = lax.associative_scan(combine, elements, axis=0)
    log_start = 0.5 * (
        jnp.log((2.0 * m_float + 1.0) / (4.0 * math.pi))
        + lax.lgamma(m_float + 0.5)
        - 0.5 * math.log(math.pi)
        - lax.lgamma(m_float + 1.0)
    )
    log_start = log_start + m_float * jnp.log(sin_theta)[None, :]
    return prefix[0] * jnp.exp(prefix[4] + log_start)


def synthesize(harmonic_slot, m_value, cos_theta, sin_theta):
    channels = harmonic_slot.shape[0]
    flat_rows = harmonic_slot.reshape(channels * 4, L)
    padded = jnp.concatenate([flat_rows, jnp.zeros_like(flat_rows)], axis=1)
    shifted = lax.dynamic_slice_in_dim(padded, m_value, L, 1)
    legendre = legendre_rows(m_value, cos_theta, sin_theta).astype(jnp.bfloat16)
    synth_maps = jnp.dot(shifted, legendre, preferred_element_type=jnp.float32)
    return synth_maps.astype(jnp.bfloat16).reshape(channels, 2, 2, cos_theta.shape[0])


def fourier_table(m_values):
    azimuth_angle = jnp.arange(NPHI, dtype=jnp.int32)
    phase_index = m_values[:, None] * azimuth_angle[None, :] % NPHI
    angle_table = phase_index.astype(jnp.float32) * (2.0 * math.pi / NPHI)
    weight = jnp.where(m_values == 0, 1.0, 2.0)[:, None]
    return jnp.stack([weight * jnp.cos(angle_table), -weight * jnp.sin(angle_table)]).astype(
        jnp.bfloat16
    )


def synthesize_slots(spherical_harmonic, m_values, cos_theta, sin_theta):

    def one_slot(slot_pair):
        return synthesize(slot_pair[0], slot_pair[1], cos_theta, sin_theta)

    return lax.map(one_slot, (spherical_harmonic, m_values))


def local(m_table, retained_modes, cycle_ids, kl_coeffs, kl_vectors, beam_matrix):
    local_modes = kl_coeffs.shape[2]
    m_all, cycles_all = (
        lax.all_gather(m_table, "ma", axis=0, tiled=True),
        lax.all_gather(cycle_ids, "ma", axis=0, tiled=True),
    )
    offset = lax.axis_index("freq") * local_modes
    mode_index = offset + jnp.arange(local_modes, dtype=jnp.int32)
    masked = jnp.where(
        mode_index[None, None, :] < retained_modes[:, None, None],
        kl_coeffs,
        jnp.zeros_like(kl_coeffs),
    )
    summed = lax.psum_scatter(
        jnp.einsum("mqn,mnck->cmqk", masked, kl_vectors, preferred_element_type=jnp.float32),
        "freq",
        scatter_dimension=0,
        tiled=True,
    )
    singular_coefficients = summed.astype(jnp.bfloat16)
    spherical_harmonic = jnp.einsum(
        "cmqk,mclk->mcql", singular_coefficients, beam_matrix, preferred_element_type=jnp.float32
    ).astype(jnp.bfloat16)
    cos_theta, sin_theta = cycle_angles(cycles_all)
    synth_block = synthesize_slots(spherical_harmonic, m_table, cos_theta, sin_theta)
    fourier = fourier_table(m_all)
    return jnp.einsum(
        "mcsqr,qmt->rsct",
        lax.all_to_all(synth_block, "ma", split_axis=4, concat_axis=0, tiled=True),
        fourier,
        preferred_element_type=jnp.float32,
    )


def solution(mesh):
    placed = (
        P("ma"),
        P("ma"),
        P("ma"),
        P("ma", None, "freq"),
        P("ma", "freq", None, None),
        P("ma", "freq", None, None),
    )
    return jax.shard_map(
        local, mesh=mesh, in_specs=placed, out_specs=P("ma", None, "freq", None), check_vma=False
    )
```

profile of v0, /device:TPU:0, one launch (start us, length us, event | category | flops | bytes accessed | tf_op | source)
XLA Modules:
  0.0 319.3 jit_solution(416983059708512161)
XLA Ops:
  4.3 8.8 %all-reduce.98 = (s32[32]{0:T(128)S(1)}, s32[8]{0:T(128)S(1)}) all-reduce(s32[32]{0:T(128)S(1)} %dynamic-update-slice.1, s32[8]{0:T(128)S(1)} %dynamic-update-slice), channel_id=1, replica_groups=mesh['ma'=4,'freq'=8] {'ma'}, use_global_device_ids=true, to_apply=%add.96 | all-reduce | flops 40 | bytes 320
  13.9 6.7 %fusion.32 = f32[32,2,4,512]{3,2,0,1:T(4,128)S(1)} fusion(bf16[2,64,32,512]{3,2,1,0:T(8,128)(2,1)} %param.12, bf16[2,4,64]{2,1,0:T(4,128)(2,1)} %param.11, pred[2,64]{1,0:T(4,128)(4,1)S(1)} %broadcast_compare_fusion), kind=kOutput, calls=%fused_computation.238 | convolution fusion | flops 16777728 | bytes 4719744 | tf_op jit(solution)/shard_map/mqn,mnck->cmqk/dot_general | solution.py:128
  20.6 34.0 %all-reduce.100 = bf16[32,2,4,512]{3,2,0,1:T(4,128)(2,1)S(1)} all-reduce(f32[32,2,4,512]{3,2,0,1:T(4,128)S(1)} %fusion.32), channel_id=2, replica_groups=mesh['ma'=4,'freq'=8] {'freq'}, use_global_device_ids=true, to_apply=%region_0.1.clone | all-reduce | flops 131072 | bytes 786432
  55.9 5.6 %convolution_convert_fusion.1 = bf16[2,4,4,1024]{3,2,1,0:T(4,128)(2,1)S(1)} fusion(bf16[2,4,1024,512]{3,2,1,0:T(8,128)(2,1)} %param.13, bf16[32,2,4,512]{3,2,0,1:T(4,128)(2,1)S(1)} %all-reduce.100, u32[]{:T(128)S(6)} %multiply.36), kind=kOutput, calls=%fused_computation.239 | convolution fusion | flops 33587200 | bytes 8486916 | tf_op jit(solution)/shard_map/cmqk,mclk->mcql/dot_general | solution.py:134
  61.6 247.0 %while.15 = (s32[]{:T(128)}, bf16[2,4,2,2,32]{4,3,2,1,0:T(2,128)(2,1)S(1)}, bf16[2,4,4,1024]{3,2,1,0:T(4,128)(2,1)S(1)}, s32[2]{0:T(128)S(1)}, f32[32]{0:T(128)S...) while((s32[]{:T(128)}, ...), condition=%wide.region_2.3_spmd, body=%wide.region_1.2_spmd.sunk | while | flops 3591383 | bytes 16577225 | solution.py:111
  63.3 2.2 slice.3169
  65.5 2.2 slice.3170
  67.7 2.2 slice.3173
  70.0 2.2 slice.3174
  72.2 2.2 slice.3171
  74.4 2.2 slice.3172
  76.6 2.7 slice.3175
  81.6 2.2 slice.3177
  83.8 2.2 slice.3178
  158.9 2.4 slice.3301
  168.1 2.2 pad.1563
  175.0 2.4 slice.3168
  177.5 2.2 pad.1561
  188.3 2.2 slice.3170
  190.5 2.2 slice.3173
  192.8 2.2 slice.3174
  195.0 2.2 slice.3171
  197.2 2.2 slice.3172
  199.4 2.4 slice.3175
  204.0 2.2 slice.3177
  206.2 2.2 slice.3178
  281.4 2.4 slice.3301
  290.6 2.2 pad.1563
  297.4 2.6 slice.3168
  300.2 2.2 pad.1561
  309.5 3.2 %all-to-all-start = ((bf16[4,2,128]{2,1,0:T(2,128)(2,1)}), bf16[4,2,128]{2,1,0:T(2,128)(2,1)S(1)}, u32[]{:S(2)}, u32[]{:S(2)}) async-start(bf16[4,2,128]{2,1,0:T(2,128)(2,1)} %reshape.286), calls=%async_computation | async-start | bytes 4096 | tf_op jit(solution)/shard_map/all_to_all | solution.py:142
  313.0 4.2 %all-to-all-done = bf16[4,2,128]{2,1,0:T(2,128)(2,1)S(1)} async-done(((bf16[4,2,128]{2,1,0:T(2,128)(2,1)}), bf16[4,2,128]{2,1,0:T(2,128)(2,1)S(1)}, u32[]{:S(2)}, u32[]{:S(2)}) %all-to-all-start) | async-done | bytes 2080 | tf_op jit(solution)/shard_map/all_to_all | solution.py:142
  (719 shorter events, 181.9 us)
Async XLA Ops:
  0.0 54.6 %copy-start.1 = (u32[32]{0:T(128)S(1)}, u32[32]{0:T(128)}, u32[]{:S(2)}) copy-start(u32[32]{0:T(128)} %constant.572) | copy-start | bytes 388
  55.9 5.7 %copy-start = (s32[2]{0:T(128)S(1)}, s32[2]{0:T(128)}, u32[]{:S(2)}) copy-start(s32[2]{0:T(128)} %param.8) | copy-start | bytes 28
  309.5 7.8 %all-to-all-start = ((bf16[4,2,128]{2,1,0:T(2,128)(2,1)}), bf16[4,2,128]{2,1,0:T(2,128)(2,1)S(1)}, u32[]{:S(2)}, u32[]{:S(2)}) async-start(bf16[4,2,128]{2,1,0:T(2,128)(2,1)} %reshape.286), calls=%async_computation | async-start | bytes 4096 | tf_op jit(solution)/shard_map/all_to_all | solution.py:142
where the time goes:
time: 325 us; the launch traced here: 319 us
  local copies, waits for them, and re-layouts  226 us (70%)
  blocking collectives  42.8 us (13%)
  loops' own time  15.6 us (5%)
  matrix products  13.1 us (4%)
  other arithmetic  12 us (4%)
  waiting for transfers between devices  4.2 us (1%)
    slice x290, local copies, waits for them, and re-layouts, legendre_rows(): prefix = lax.associative_scan(combine, elements, axis=0)  156 us
    pad x156, local copies, waits for them, and re-layouts, legendre_rows(): prefix = lax.associative_scan(combine, elements, axis=0)  56.4 us
    unnamed x2, blocking collectives  42.8 us
    another operation x1, loops' own time, synthesize_slots(): return lax.map(one_slot, (spherical_harmonic, m_values))  15.6 us
    while x6, local copies, waits for them, and re-layouts  6.79 us
    dot_general x1, matrix products, local(): jnp.einsum('mqn,mnck->cmqk', masked, kl_vectors, preferred_element_type=j...  6.71 us
  transfers between devices with their start and end apart: 1, of which 1 were waited for; matrix products, arithmetic and copies ran while one was open for 0% of the time, Pallas kernels for 0%

commit v1 on v0

v1 whole, which is shorter than its diff:
```python
import functools
import math

import jax
import jax.numpy as jnp
from jax import lax
from jax.experimental import pallas as pl
from jax.experimental.pallas import tpu as pltpu
from jax.sharding import PartitionSpec as P

NPHI = 2048
L = 1024
NSIDE = 512
PARTS = 4
BLOCKS = 32
STEPS = L // BLOCKS
ROWS = 256
LANES = 128
GROUP = 16

f32 = jnp.float32
bf16 = jnp.bfloat16
VMEM = pl.BlockSpec(memory_space=pltpu.VMEM)
SMEM = pl.BlockSpec(memory_space=pltpu.SMEM)
HBM = pl.BlockSpec(memory_space=pl.ANY)
LIMIT = 48 * 1024 * 1024


def padded(width):
    return -(-width // LANES) * LANES


def iota(shape, axis):
    return lax.broadcasted_iota(jnp.int32, shape, axis)


def kl_kernel(offset_ref, kept_ref, coeff_ref, vectors_hbm, out_ref, held, spread, sems):
    slots, modes, channels, depth = vectors_hbm.shape
    group = min(GROUP, channels)
    pieces = out_ref.shape[0]
    share = channels // pieces

    def copy(s):
        return pltpu.make_async_copy(vectors_hbm.at[s], held.at[s], sems.at[s])

    for s in range(slots):
        copy(s).start()
    rows, columns = group * PARTS, modes * group
    expand = (iota((modes, columns), 1) // group == iota((modes, columns), 0)).astype(bf16)
    mode_index = offset_ref[0] + iota((PARTS, modes), 1)
    keep = iota((rows, columns), 1) % group == iota((rows, columns), 0) // PARTS
    for s in range(slots):
        masked = jnp.where(mode_index < kept_ref[s], coeff_ref[s].astype(f32), 0.0)
        tall = jnp.concatenate([masked] * group, axis=0).astype(bf16)
        wide = jnp.dot(tall, expand, preferred_element_type=f32)
        spread[s] = jnp.where(keep, wide, 0.0).astype(bf16)
    for s in range(slots):
        copy(s).wait()
        for g in range(channels // group):
            block = held[s, :, g * group : (g + 1) * group, :].reshape(columns, depth)
            sums = jnp.dot(spread[s], block, preferred_element_type=f32).astype(bf16)
            for i in range(group // share):
                out_ref[g * (group // share) + i, s] = sums[
                    i * share * PARTS : (i + 1) * share * PARTS
                ]


def kl_stage(offset, kept, coeffs, vectors, pieces):
    slots, modes, channels, depth = vectors.shape
    group = min(GROUP, channels)
    return pl.pallas_call(
        kl_kernel,
        out_shape=jax.ShapeDtypeStruct(
            (pieces, slots, channels // pieces * PARTS, depth), bf16
        ),
        in_specs=[SMEM, SMEM, VMEM, HBM],
        out_specs=VMEM,
        scratch_shapes=[
            pltpu.VMEM((slots, modes, channels, depth), bf16),
            pltpu.VMEM((slots, group * PARTS, modes * group), bf16),
            pltpu.SemaphoreType.DMA((slots,)),
        ],
        compiler_params=pltpu.CompilerParams(vmem_limit_bytes=LIMIT),
        name="kl_stage",
    )(offset, kept, coeffs, vectors)


def angles(cycle):
    n = float(NSIDE)
    p = jnp.minimum(cycle, 4.0 * n - cycle)
    t = p * p / (3.0 * n * n)
    cap_sin = p * (1.0 / (math.sqrt(3.0) * n)) * jnp.sqrt(2.0 - t)
    belt_cos = 4.0 / 3.0 - p * (2.0 / (3.0 * n))
    belt_sin = jnp.sqrt(jnp.maximum(1.0 - belt_cos * belt_cos, 0.25))
    cap = p < n
    cosine = jnp.where(cap, 1.0 - t, belt_cos)
    return jnp.where(cycle <= 2.0 * n, cosine, -cosine), jnp.where(cap, cap_sin, belt_sin)


def log2_start(m, sine):
    x = m + 4.25
    y = 1.0 / (x * x)
    series = 1.0 + y * (-1.0 / 64.0 + y * (21.0 / 8192.0 - y * (671.0 / 524288.0)))
    product = series * lax.rsqrt(x) * (1.0 / math.sqrt(math.pi))
    for k in range(1, 5):
        product = product * ((m + k) / (m + (k - 0.5)))
    scale = (2.0 * m + 1.0) * (1.0 / (4.0 * math.pi)) * product
    return (0.5 * jnp.log(scale) + m * jnp.log(sine)) * (1.0 / math.log(2.0))


def legendre_rows(m, cosine, sine, p_ref, q_ref, left, right, scale, table):
    width = m.shape[1]
    first = (iota((BLOCKS, width), 0) * STEPS).astype(f32)
    m_all = jnp.broadcast_to(m, (BLOCKS, width))
    c_all = jnp.broadcast_to(cosine, (BLOCKS, width))
    began = first > m_all
    p1 = jnp.where(began, 1.0, 0.0)
    p0 = jnp.zeros_like(p1)
    q1 = jnp.zeros_like(p1)
    q0 = p1

    def factors(l):
        over = (l - m_all) * (l + m_all)
        under = 4.0 * l * l - 1.0
        root = lax.rsqrt(jnp.maximum(over, 1.0) * jnp.maximum(under, 1.0))
        live = over > 0.0
        return jnp.where(live, under * root, 0.0), jnp.where(live, over * root, 0.0)

    _, last_inverse = factors(first - 1.0)
    last_inverse = jnp.where(began, last_inverse, 0.0)
    for i in range(STEPS):
        l = first + float(i)
        a, inverse = factors(l)
        above = l > m_all
        a = jnp.where(above, a, 0.0)
        rise = a * c_all
        fall = a * last_inverse
        p2 = rise * p1 - fall * p0
        q2 = rise * q1 - fall * q0
        p2 = jnp.where(l == m_all, 1.0, p2)
        p1, p0 = p2, p1
        q1, q0 = q2, q1
        last_inverse = jnp.where(above, inverse, 0.0)
        p_ref[i] = p2
        q_ref[i] = q2

    size = jnp.maximum(
        jnp.maximum(jnp.abs(p1), jnp.abs(p0)), jnp.maximum(jnp.abs(q1), jnp.abs(q0))
    )
    power = jnp.floor(jnp.log(jnp.maximum(size, 1.0)) * (1.0 / math.log(2.0)))
    power = jnp.where(power >= 20.0, power, 0.0)
    shrink = jnp.exp2(-power)
    p1, p0, q1, q0 = p1 * shrink, p0 * shrink, q1 * shrink, q0 * shrink

    start = log2_start(m, sine)
    start_power = jnp.floor(start)
    start_value = jnp.exp2(start - start_power)
    here = jnp.zeros((1, width), f32)
    before = jnp.zeros((1, width), f32)
    level = jnp.zeros((1, width), f32)
    for b in range(BLOCKS):
        enters = (m >= float(b * STEPS)) & (m < float((b + 1) * STEPS))
        here = jnp.where(enters, start_value, here)
        before = jnp.where(enters, 0.0, before)
        level = jnp.where(enters, start_power, level)
        left[b : b + 1] = here
        right[b : b + 1] = before
        scale[b : b + 1] = level
        here, before = (
            p1[b : b + 1] * here + q1[b : b + 1] * before,
            p0[b : b + 1] * here + q0[b : b + 1] * before,
        )
        large = jnp.maximum(jnp.abs(here), jnp.abs(before)) > 2.0**30
        factor = jnp.where(large, 2.0**-30, 1.0)
        here = here * factor
        before = before * factor
        level = level + power[b : b + 1] + jnp.where(large, 30.0, 0.0)

    half = jnp.exp2(jnp.maximum(scale[...] * 0.5, -120.0))
    from_left = left[...] * half
    from_right = right[...] * half
    for i in range(STEPS):
        rows = (from_left * p_ref[i] + from_right * q_ref[i]) * half
        for j in range(width // LANES):
            table[j, pl.ds(i, BLOCKS, stride=STEPS), :] = rows[:, j * LANES : (j + 1) * LANES]


def sine_quarter(z):
    x = z * (2.0 * math.pi)
    y = x * x
    return x * (
        1.0
        + y
        * (
            -1.0 / 6.0
            + y * (1.0 / 120.0 + y * (-1.0 / 5040.0 + y * (1.0 / 362880.0 - y / 39916800.0)))
        )
    )


def fourier_rows(m):
    turn = (m * iota((m.shape[0], NPHI), 1)) % NPHI
    z = turn.astype(f32) * (1.0 / NPHI)
    z = jnp.where(z >= 0.5, z - 1.0, z)
    size = jnp.abs(z)
    cosine = sine_quarter(0.25 - size)
    folded = sine_quarter(jnp.where(size > 0.25, 0.5 - size, size))
    sine = jnp.where(z < 0.0, -folded, folded)
    weight = jnp.where(m == 0, 1.0, 2.0)
    return weight * cosine, -weight * sine


def projection_kernel(
    m_ref, ids_ref, beam_hbm, folded_ref, fourier_ref,
    held, p_ref, q_ref, left, right, scale, table, turned, sums, woven, sems,
):
    slots, share, _, depth = beam_hbm.shape
    members, entries = ids_ref.shape
    cycles_each = entries - slots
    cycles = members * cycles_each
    pieces = L // ROWS

    def copy(s, t):
        return pltpu.make_async_copy(
            beam_hbm.at[s, :, pl.ds(t * ROWS, ROWS), :],
            held.at[s, :, pl.ds(t * ROWS, ROWS), :],
            sems.at[s, t],
        )

    def needed(s, t):
        return m_ref[s] < (t + 1) * ROWS

    for t in reversed(range(pieces)):
        for s in range(slots):
            pl.when(needed(s, t))(copy(s, t).start)

    width = padded(slots * cycles)
    lane = iota((1, width), 1)
    m = jnp.zeros((1, width), jnp.int32)
    for s in range(slots):
        m = jnp.where(lane // cycles == s, m_ref[s], m)
    cycle = jnp.zeros((1, width), jnp.int32)
    for a in range(members):
        for r in range(cycles_each):
            cycle = jnp.where(lane % cycles == a * cycles_each + r, ids_ref[a, slots + r], cycle)
    cosine, sine = angles(cycle.astype(f32))
    legendre_rows(m.astype(f32), cosine, sine, p_ref, q_ref, left, right, scale, table)
    for j in range(width // LANES):
        turned[j * LANES : (j + 1) * LANES] = table[j].T.astype(bf16)

    every = members * slots
    row = iota((every, 1), 0)
    m_every = jnp.zeros((every, 1), jnp.int32)
    for a in range(members):
        for s in range(slots):
            m_every = jnp.where(row == a * slots + s, ids_ref[a, s], m_every)
    real, imaginary = fourier_rows(m_every)
    fourier_ref[:every] = real.astype(bf16)
    fourier_ref[every:] = imaginary.astype(bf16)

    sums[...] = jnp.zeros_like(sums)
    for t in reversed(range(pieces)):
        for s in range(slots):

            @pl.when(needed(s, t))
            def _():
                copy(s, t).wait()
                lhs = turned[s * cycles : (s + 1) * cycles, t * ROWS : (t + 1) * ROWS]
                for c in range(share):
                    sums[s, c] += jnp.dot(
                        lhs, held[s, c, t * ROWS : (t + 1) * ROWS, :], preferred_element_type=f32
                    )

    for s in range(slots):
        for c in range(share):
            for j in range(depth // LANES):
                woven[s, j, pl.ds(c, cycles, stride=share), :] = sums[
                    s, c, :, j * LANES : (j + 1) * LANES
                ]
        for j in range(depth // LANES):
            folded_ref[s, :, j * LANES : (j + 1) * LANES] = woven[s, j].astype(bf16)


def projection(m_table, ids, beam):
    slots, share, _, depth = beam.shape
    members, entries = ids.shape
    cycles = members * (entries - slots)
    width = padded(slots * cycles)
    every = members * slots
    return pl.pallas_call(
        projection_kernel,
        out_shape=(
            jax.ShapeDtypeStruct((slots, cycles * share, depth), bf16),
            jax.ShapeDtypeStruct((2 * every, NPHI), bf16),
        ),
        in_specs=[SMEM, SMEM, HBM],
        out_specs=(VMEM, VMEM),
        scratch_shapes=[
            pltpu.VMEM((slots, share, L, depth), bf16),
            pltpu.VMEM((STEPS, BLOCKS, width), f32),
            pltpu.VMEM((STEPS, BLOCKS, width), f32),
            pltpu.VMEM((BLOCKS, width), f32),
            pltpu.VMEM((BLOCKS, width), f32),
            pltpu.VMEM((BLOCKS, width), f32),
            pltpu.VMEM((width // LANES, L, LANES), f32),
            pltpu.VMEM((width, L), bf16),
            pltpu.VMEM((slots, share, cycles, depth), f32),
            pltpu.VMEM((slots, depth // LANES, cycles * share, LANES), f32),
            pltpu.SemaphoreType.DMA((slots, L // ROWS)),
        ],
        compiler_params=pltpu.CompilerParams(vmem_limit_bytes=LIMIT),
        name="projection",
    )(m_table, ids, beam)


def cycle_kernel(parts_ref, folded_ref, out_ref):
    members, rows, columns = out_ref.shape
    slots = folded_ref.shape[0]
    per_slot = columns // slots
    share = per_slot // PARTS
    total = parts_ref[0].astype(f32)
    for i in range(1, parts_ref.shape[0]):
        total = total + parts_ref[i].astype(f32)
    singular = total.reshape(columns, total.shape[-1]).astype(bf16)
    shape = (members * rows, columns)
    values = jnp.zeros(shape, f32)
    for s in range(slots):
        product = lax.dot_general(
            folded_ref[s], singular, (((1,), (1,)), ((), ())),
            preferred_element_type=f32,
        )
        values = jnp.where(iota(shape, 1) // per_slot == s, product, values)
    same = iota(shape, 0) % share == (iota(shape, 1) // PARTS) % share
    values = jnp.where(same, values, 0.0).astype(bf16)
    for a in range(members):
        out_ref[a] = values[a * rows : (a + 1) * rows]


def cycle_values(parts, folded, members):
    _, slots, per_slot, _ = parts.shape
    rows = folded.shape[1] // members
    return pl.pallas_call(
        cycle_kernel,
        out_shape=jax.ShapeDtypeStruct((members, rows, slots * per_slot), bf16),
        in_specs=[VMEM, VMEM],
        out_specs=VMEM,
        compiler_params=pltpu.CompilerParams(vmem_limit_bytes=LIMIT),
        name="cycle_values",
    )(parts, folded)


def sky_kernel(values_ref, fourier_ref, out_ref):
    members, rows, columns = values_ref.shape
    every = fourier_ref.shape[0] // 2
    slots = every // members
    per_slot = columns // slots
    share = per_slot // PARTS
    shape = (columns, 2 * every)
    part = iota(shape, 0) % PARTS
    slot = iota(shape, 0) // per_slot
    target = iota(shape, 1)
    for d in range(2):
        folded = jnp.zeros((rows, 2 * every), f32)
        for a in range(members):
            choose = (part // 2 == d) & (target == (part % 2) * every + a * slots + slot)
            folded = folded + jnp.dot(
                values_ref[a], jnp.where(choose, 1.0, 0.0).astype(bf16), preferred_element_type=f32
            )
        maps = jnp.dot(folded.astype(bf16), fourier_ref[...], preferred_element_type=f32)
        out_ref[:, d] = maps.reshape(rows // share, share, NPHI)


def sky_maps(values, fourier, share):
    members, rows, columns = values.shape
    return pl.pallas_call(
        sky_kernel,
        out_shape=jax.ShapeDtypeStruct((rows // share, 2, share, NPHI), f32),
        in_specs=[VMEM, VMEM],
        out_specs=VMEM,
        compiler_params=pltpu.CompilerParams(vmem_limit_bytes=LIMIT),
        name="sky_maps",
    )(values, fourier)


def local(members, pieces, m_table, retained_modes, cycle_ids, kl_coeffs, kl_vectors, beam_matrix):
    ids = lax.all_gather(jnp.concatenate([m_table, cycle_ids]), "ma", axis=0, tiled=False)
    offset = (lax.axis_index("freq") * kl_coeffs.shape[2]).astype(jnp.int32).reshape(1)
    sums = kl_stage(offset, retained_modes, kl_coeffs, kl_vectors, pieces)
    parts = lax.all_to_all(sums, "freq", split_axis=0, concat_axis=0, tiled=True)
    folded, fourier = projection(m_table, ids, beam_matrix)
    values = cycle_values(parts, folded, members)
    values = lax.all_to_all(values, "ma", split_axis=0, concat_axis=0, tiled=True)
    return sky_maps(values, fourier, beam_matrix.shape[1])


def solution(mesh):
    placed = (
        P("ma"),
        P("ma"),
        P("ma"),
        P("ma", None, "freq"),
        P("ma", "freq", None, None),
        P("ma", "freq", None, None),
    )
    return jax.shard_map(
        functools.partial(local, mesh.shape["ma"], mesh.shape["freq"]),
        mesh=mesh,
        in_specs=placed,
        out_specs=P("ma", None, "freq", None),
        check_vma=False,
    )
```

time: 325 us -> 36.6 us (0.11); the launches traced: 319 us -> 36.3 us
  local copies, waits for them, and re-layouts: 226 us -> 5.7 us
  blocking collectives: 42.8 us -> 14.6 us
  loops' own time: 15.6 us -> 0 us
  matrix products: 13.1 us -> 0 us
  other arithmetic: 12 us -> 0.84 us
  Pallas kernels: 0 us -> 8.03 us
  waiting for transfers between devices: 4.2 us -> 0.01 us
    slice x290 -> x0, local copies, waits for them, and re-layouts: 156 us -> none  [legendre_rows(): prefix = lax.associative_scan(combine, elements, axis=0)]
    pad x156 -> x0, local copies, waits for them, and re-layouts: 56.4 us -> none  [legendre_rows(): prefix = lax.associative_scan(combine, elements, axis=0)]
    unnamed x2 -> x1, blocking collectives: 42.8 us -> 7.37 us
    another operation x1 -> x0, loops' own time: 15.6 us -> none  [synthesize_slots(): return lax.map(one_slot, (spherical_harmonic, m_values))]
    dot_general x5 -> x0, matrix products: 13.1 us -> none  [the longest x1 6.71 us: local(): jnp.einsum('mqn,mnck->cmqk', masked, kl_vectors, preferred_element_type=j...]
    pallas_call x0 -> x4, Pallas kernels: none -> 8.03 us  [the longest x1 3.79 us: projection(): pl.pallas_call(projection_kernel, out_shape=(jax.ShapeDtypeStruct((slots,...]
    all_to_all x0 -> x1, blocking collectives: none -> 7.26 us  [local(): lax.all_to_all(values, 'ma', split_axis=0, concat_axis=0, tiled=True)]
    while x7 -> x0, local copies, waits for them, and re-layouts: 6.93 us -> none
  transfers between devices with their start and end apart: 1 -> 1, of which waited for: 1 -> 0; matrix products, arithmetic and copies ran while one was open for 0% -> 6% of each run, Pallas kernels for 0% -> 10%
where the time goes in v1:
time: 36.6 us; the launch traced here: 36.3 us
  blocking collectives  14.6 us (40%)
  Pallas kernels  8.03 us (22%)
  starting transfers between devices  6.37 us (17%)
  local copies, waits for them, and re-layouts  5.7 us (16%)
  other arithmetic  0.84 us (2%)
  between operations  0.67 us (2%)
    unnamed x1, blocking collectives  7.37 us
    all_to_all x1, blocking collectives, local(): lax.all_to_all(values, 'ma', split_axis=0, concat_axis=0, tiled=True)  7.26 us
    all_to_all x1, starting transfers between devices, local(): lax.all_to_all(sums, 'freq', split_axis=0, concat_axis=0, tiled=True)  6.37 us
    unnamed x12, local copies, waits for them, and re-layouts  5.62 us
    pallas_call x1, Pallas kernels, projection(): pl.pallas_call(projection_kernel, out_shape=(jax.ShapeDtypeStruct((slots,...  3.79 us
    pallas_call x1, Pallas kernels, kl_stage(): pl.pallas_call(kl_kernel, out_shape=jax.ShapeDtypeStruct((pieces, slots,...  2.71 us
    pallas_call x1, Pallas kernels, sky_maps(): pl.pallas_call(sky_kernel, out_shape=jax.ShapeDtypeStruct((rows // share,...  1.31 us
    unnamed x1, other arithmetic  0.84 us
  transfers between devices with their start and end apart: 1, of which 0 were waited for; matrix products, arithmetic and copies ran while one was open for 6% of the time, Pallas kernels for 10%

profile of v1, /device:TPU:0, one launch (start us, length us, event | category | flops | bytes accessed | tf_op | source)
XLA Modules:
  0.0 36.3 jit_solution(5901149658899027311)
XLA Ops:
  0.0 0.0 copy-start
  0.0 2.2 %copy-done = bf16[2,64,32,512]{3,2,1,0:T(8,128)(2,1)S(1)} copy-done((bf16[2,64,32,512]{3,2,1,0:T(8,128)(2,1)S(1)}, bf16[2,64,32,512]{3,2,1,0:T(8,128)(2,1)}, u32[]{:S(2)}) %copy-start) | copy-done | bytes 4194328
  2.2 0.0 copy-start.1
  2.2 0.7 %copy-done.1 = bf16[2,4,64]{2,1,0:T(4,128)(2,1)S(1)} copy-done((bf16[2,4,64]{2,1,0:T(4,128)(2,1)S(1)}, bf16[2,4,64]{2,1,0:T(4,128)(2,1)}, u32[]{:S(2)}) %copy-start.1) | copy-done | bytes 1048
  2.9 0.0 copy-start.3
  2.9 0.7 %copy-done.3 = s32[2]{0:T(128)S(1)} copy-done((s32[2]{0:T(128)S(1)}, s32[2]{0:T(128)}, u32[]{:S(2)}) %copy-start.3) | copy-done | bytes 32
  3.5 2.7 %kl_stage.1 = bf16[8,2,16,512]{3,2,1,0:T(8,128)(2,1)} custom-call(s32[1]{0:T(128)} %bitcast.offset_ref, s32[2]{0:T(128)S(1)} %copy-done.3, bf16[2,4,64]{2,1,0:T(4,128)(2,1)S(1)} %copy-done.1, bf16[2,64,32,512]{3,2,1,0:T(8,128)(2,1)S(1)} %copy-done), custom_call_target="tpu_custom_call" | custom-call | tf_op jit(solution)/shard_map/kl_stage/pallas_call | solution.py:71
  6.2 6.4 %all-to-all-start = ((bf16[8,2,16,512]{3,2,1,0:T(8,128)(2,1)}), bf16[8,2,16,512]{3,2,1,0:T(8,128)(2,1)S(1)}, u32[]{:S(2)}, u32[]{:S(2)}) async-start(bf16[8,2,16,512]{3,2,1,0:T(8,128)(2,1)} %kl_stage.1), calls=%async_computation | async-start | bytes 524288 | tf_op jit(solution)/shard_map/all_to_all | solution.py:389
  12.6 1.2 %dynamic-slice = u32[1]{0:T(128)} dynamic-slice(u32[32]{0:T(128)} %constant.13, u32[]{:T(128)S(6)} %add), dynamic_slice_sizes={1} | dynamic-slice | bytes 12
  14.5 0.8 %add_dynamic-update-slice_fusion = s32[40]{0:T(128)S(1)} fusion(s32[40]{0:T(128)S(1)} %broadcast, u32[]{:T(128)} %bitcast.1, s32[8]{0:T(128)} %param.8, s32[2]{0:T(128)} %m_ref.1), kind=kLoop, calls=%fused_computation | loop fusion | flops 10 | bytes 204
  15.3 7.4 %all-reduce = s32[40]{0:T(128)S(1)} all-reduce(s32[40]{0:T(128)S(1)} %add_dynamic-update-slice_fusion), channel_id=2, replica_groups=mesh['ma'=4,'freq'=8] {'ma'}, use_global_device_ids=true, to_apply=%add | all-reduce | flops 40 | bytes 320
  22.7 0.1 reshape.4.ids_ref
  22.8 0.0 copy-start.2
  22.8 0.7 %copy-done.2 = s32[2]{0:T(128)S(1)} copy-done((s32[2]{0:T(128)S(1)}, s32[2]{0:T(128)}, u32[]{:S(2)}) %copy-start.2) | copy-done | bytes 32
  23.4 3.8 %projection.1 = (bf16[2,128,512]{2,1,0:T(8,128)(2,1)S(1)}, bf16[16,2048]{1,0:T(8,128)(2,1)S(1)}) custom-call(s32[2]{0:T(128)S(1)} %copy-done.2, s32[4,10]{1,0:T(4,128)S(1)} %reshape.4.ids_ref, bf16[2,4,1024,512]{3,2,1,0:T(8,128)(2,1)} %beam_hbm.1), custom_call_target="tpu_custom_call" | custom-call | tf_op jit(solution)/shard_map/projection/pallas_call | solution.py:290
  27.2 0.0 all-to-all-done.parts_ref
  27.3 0.2 cycle_values.1
  27.5 0.1 reshape.10
  27.6 7.3 %all_to_all.10 = bf16[4,2,512]{2,1,0:T(2,128)(2,1)S(1)} all-to-all(bf16[4,2,512]{2,1,0:T(2,128)(2,1)S(1)} %reshape.10), channel_id=1, replica_groups=mesh['ma'=4,'freq'=8] {'ma'}, dimensions={0} | all-to-all | bytes 16384 | tf_op jit(solution)/shard_map/all_to_all | solution.py:392
  34.9 0.1 reshape.11.values_ref
  34.9 1.3 %sky_maps.1 = f32[8,2,4,2048]{3,2,1,0:T(4,128)} custom-call(bf16[4,32,32]{2,1,0:T(8,128)(2,1)S(1)} %reshape.11.values_ref, bf16[16,2048]{1,0:T(8,128)(2,1)S(1)} %get-tuple-element.8.fourier_ref), custom_call_target="tpu_custom_call" | custom-call | tf_op jit(solution)/shard_map/sky_maps/pallas_call | solution.py:375
  (1 shorter events, 0.0 us)
Async XLA Ops:
  0.0 2.2 %copy-start = (bf16[2,64,32,512]{3,2,1,0:T(8,128)(2,1)S(1)}, bf16[2,64,32,512]{3,2,1,0:T(8,128)(2,1)}, u32[]{:S(2)}) copy-start(bf16[2,64,32,512]{3,2,1,0:T(8,128)(2,1)} %vectors_hbm.1) | copy-start | bytes 12582916
  2.2 0.7 %copy-start.1 = (bf16[2,4,64]{2,1,0:T(4,128)(2,1)S(1)}, bf16[2,4,64]{2,1,0:T(4,128)(2,1)}, u32[]{:S(2)}) copy-start(bf16[2,4,64]{2,1,0:T(4,128)(2,1)} %coeff_ref.1) | copy-start | bytes 3076
  2.9 0.7 %copy-start.3 = (s32[2]{0:T(128)S(1)}, s32[2]{0:T(128)}, u32[]{:S(2)}) copy-start(s32[2]{0:T(128)} %kept_ref.1) | copy-start | bytes 28
  6.2 21.0 %all-to-all-start = ((bf16[8,2,16,512]{3,2,1,0:T(8,128)(2,1)}), bf16[8,2,16,512]{3,2,1,0:T(8,128)(2,1)S(1)}, u32[]{:S(2)}, u32[]{:S(2)}) async-start(bf16[8,2,16,512]{3,2,1,0:T(8,128)(2,1)} %kl_stage.1), calls=%async_computation | async-start | bytes 524288 | tf_op jit(solution)/shard_map/all_to_all | solution.py:389
  22.8 0.7 %copy-start.2 = (s32[2]{0:T(128)S(1)}, s32[2]{0:T(128)}, u32[]{:S(2)}) copy-start(s32[2]{0:T(128)} %m_ref.1) | copy-start | bytes 28

commit v2 on v1

--- a/solution.py
+++ b/solution.py
@@ -7,6 +7,7 @@
 from jax.experimental import pallas as pl
 from jax.experimental.pallas import tpu as pltpu
 from jax.sharding import PartitionSpec as P
+
 
 NPHI = 2048
 L = 1024
@@ -18,12 +19,14 @@
 LANES = 128
 GROUP = 16
 
+
 f32 = jnp.float32
 bf16 = jnp.bfloat16
 VMEM = pl.BlockSpec(memory_space=pltpu.VMEM)
 SMEM = pl.BlockSpec(memory_space=pltpu.SMEM)
-HBM = pl.BlockSpec(memory_space=pl.ANY)
-LIMIT = 48 * 1024 * 1024
+HBM = pl.BlockSpec(memory_space=pltpu.HBM)
+LIMIT = 16 * 1024 * 1024
+SMALL = 2 * 1024 * 1024
 
 
 def padded(width):
@@ -34,55 +37,111 @@
     return lax.broadcasted_iota(jnp.int32, shape, axis)
 
 
-def kl_kernel(offset_ref, kept_ref, coeff_ref, vectors_hbm, out_ref, held, spread, sems):
-    slots, modes, channels, depth = vectors_hbm.shape
+def work(microseconds):
+    return pl.CostEstimate(
+        flops=int(microseconds * 1e9), transcendentals=0, bytes_accessed=4096
+    )
+
+
+def kl_kernel(kept_ref, coeff_ref, vectors_ref, keep_ref, send_ref, spread, ready):
+    slots, modes, channels, depth = vectors_ref.shape
     group = min(GROUP, channels)
-    pieces = out_ref.shape[0]
+    pieces = keep_ref.shape[0] * 2
     share = channels // pieces
-
-    def copy(s):
-        return pltpu.make_async_copy(vectors_hbm.at[s], held.at[s], sems.at[s])
-
-    for s in range(slots):
-        copy(s).start()
+    place = lax.axis_index("freq")
     rows, columns = group * PARTS, modes * group
     expand = (iota((modes, columns), 1) // group == iota((modes, columns), 0)).astype(bf16)
-    mode_index = offset_ref[0] + iota((PARTS, modes), 1)
-    keep = iota((rows, columns), 1) % group == iota((rows, columns), 0) // PARTS
+    mode_index = place * modes + iota((PARTS, modes), 1)
+    diagonal = iota((rows, columns), 1) % group == iota((rows, columns), 0) // PARTS
     for s in range(slots):
         masked = jnp.where(mode_index < kept_ref[s], coeff_ref[s].astype(f32), 0.0)
         tall = jnp.concatenate([masked] * group, axis=0).astype(bf16)
         wide = jnp.dot(tall, expand, preferred_element_type=f32)
-        spread[s] = jnp.where(keep, wide, 0.0).astype(bf16)
+        spread[s] = jnp.where(diagonal, wide, 0.0).astype(bf16)
+    parity = place % 2
     for s in range(slots):
-        copy(s).wait()
         for g in range(channels // group):
-            block = held[s, :, g * group : (g + 1) * group, :].reshape(columns, depth)
-            sums = jnp.dot(spread[s], block, preferred_element_type=f32).astype(bf16)
+            block = vectors_ref[s, :, g * group : (g + 1) * group, :].reshape(columns, depth)
+            sums = jnp.dot(spread[s], block, preferred_element_type=f32)
             for i in range(group // share):
-                out_ref[g * (group // share) + i, s] = sums[
+                piece = g * (group // share) + i
+                ready[(piece + parity) % 2, piece // 2, s] = sums[
                     i * share * PARTS : (i + 1) * share * PARTS
                 ]
-
-
-def kl_stage(offset, kept, coeffs, vectors, pieces):
+    keep_ref[...] = ready[0]
+    send_ref[...] = ready[1].astype(bf16)
+
+
+def kl_stage(kept, coeffs, vectors, pieces):
     slots, modes, channels, depth = vectors.shape
     group = min(GROUP, channels)
+    shape = (pieces // 2, slots, channels // pieces * PARTS, depth)
     return pl.pallas_call(
         kl_kernel,
-        out_shape=jax.ShapeDtypeStruct(
-            (pieces, slots, channels // pieces * PARTS, depth), bf16
-        ),
-        in_specs=[SMEM, SMEM, VMEM, HBM],
+        out_shape=(jax.ShapeDtypeStruct(shape, f32), jax.ShapeDtypeStruct(shape, bf16)),
+        in_specs=[SMEM, VMEM, VMEM],
+        out_specs=(VMEM, VMEM),
+        scratch_shapes=[
+            pltpu.VMEM((slots, group * PARTS, modes * group), bf16),
+            pltpu.VMEM((2, *shape), f32),
+        ],
+        compiler_params=pltpu.CompilerParams(vmem_limit_bytes=LIMIT),
+        cost_estimate=work(2.0),
+        name="kl_stage",
+    )(kept, coeffs, vectors)
+
+
+def fold_kernel(bit, held_ref, got_ref, keep_ref, send_ref):
+    mine = (lax.axis_index("freq") // bit) % 2
+    for i in range(keep_ref.shape[0]):
+        keep_ref[i] = held_ref[2 * i + mine] + got_ref[2 * i + mine].astype(f32)
+        other = 2 * i + 1 - mine
+        send_ref[i] = (held_ref[other] + got_ref[other].astype(f32)).astype(bf16)
+
+
+def fold_stage(bit, held, got):
+    shape = (held.shape[0] // 2, *held.shape[1:])
+    return pl.pallas_call(
+        functools.partial(fold_kernel, bit),
+        out_shape=(jax.ShapeDtypeStruct(shape, f32), jax.ShapeDtypeStruct(shape, bf16)),
+        in_specs=[VMEM, VMEM],
+        out_specs=(VMEM, VMEM),
+        compiler_params=pltpu.CompilerParams(vmem_limit_bytes=LIMIT),
+        name="fold_stage",
+    )(held, got)
+
+
+def stack_kernel(low_ref, high_ref, out_ref):
+    rows = low_ref.shape[0]
+    out_ref[:rows] = low_ref[...]
+    out_ref[rows:] = high_ref[...]
+
+
+def copy_kernel(in_ref, out_ref):
+    out_ref[...] = in_ref[...]
+
+
+def lead(value):
+    return pl.pallas_call(
+        copy_kernel,
+        out_shape=jax.ShapeDtypeStruct(value.shape, value.dtype),
+        in_specs=[VMEM],
         out_specs=VMEM,
-        scratch_shapes=[
-            pltpu.VMEM((slots, modes, channels, depth), bf16),
-            pltpu.VMEM((slots, group * PARTS, modes * group), bf16),
-            pltpu.SemaphoreType.DMA((slots,)),
-        ],
-        compiler_params=pltpu.CompilerParams(vmem_limit_bytes=LIMIT),
-        name="kl_stage",
-    )(offset, kept, coeffs, vectors)
+        compiler_params=pltpu.CompilerParams(vmem_limit_bytes=SMALL),
+        cost_estimate=work(4.0),
+        name="lead",
+    )(value)
+
+
+def stack(low, high):
+    return pl.pallas_call(
+        stack_kernel,
+        out_shape=jax.ShapeDtypeStruct((2 * low.shape[0], low.shape[1]), low.dtype),
+        in_specs=[VMEM, VMEM],
+        out_specs=VMEM,
+        compiler_params=pltpu.CompilerParams(vmem_limit_bytes=SMALL),
+        name="stack",
+    )(low, high)
 
 
 def angles(cycle):
@@ -210,35 +269,17 @@
     return weight * cosine, -weight * sine
 
 
-def projection_kernel(
-    m_ref, ids_ref, beam_hbm, folded_ref, fourier_ref,
-    held, p_ref, q_ref, left, right, scale, table, turned, sums, woven, sems,
+def legendre_kernel(
+    slots, ids_ref, turned_ref, fourier_ref, p_ref, q_ref, left, right, scale, table
 ):
-    slots, share, _, depth = beam_hbm.shape
     members, entries = ids_ref.shape
     cycles_each = entries - slots
     cycles = members * cycles_each
-    pieces = L // ROWS
-
-    def copy(s, t):
-        return pltpu.make_async_copy(
-            beam_hbm.at[s, :, pl.ds(t * ROWS, ROWS), :],
-            held.at[s, :, pl.ds(t * ROWS, ROWS), :],
-            sems.at[s, t],
-        )
-
-    def needed(s, t):
-        return m_ref[s] < (t + 1) * ROWS
-
-    for t in reversed(range(pieces)):
-        for s in range(slots):
-            pl.when(needed(s, t))(copy(s, t).start)
-
     width = padded(slots * cycles)
     lane = iota((1, width), 1)
     m = jnp.zeros((1, width), jnp.int32)
     for s in range(slots):
-        m = jnp.where(lane // cycles == s, m_ref[s], m)
+        m = jnp.where(lane // cycles == s, ids_ref[0, s], m)
     cycle = jnp.zeros((1, width), jnp.int32)
     for a in range(members):
         for r in range(cycles_each):
@@ -246,7 +287,7 @@
     cosine, sine = angles(cycle.astype(f32))
     legendre_rows(m.astype(f32), cosine, sine, p_ref, q_ref, left, right, scale, table)
     for j in range(width // LANES):
-        turned[j * LANES : (j + 1) * LANES] = table[j].T.astype(bf16)
+        turned_ref[j * LANES : (j + 1) * LANES] = table[j].T.astype(bf16)
 
     every = members * slots
     row = iota((every, 1), 0)
@@ -258,17 +299,46 @@
     fourier_ref[:every] = real.astype(bf16)
     fourier_ref[every:] = imaginary.astype(bf16)
 
+
+def legendre_stage(ids, slots):
+    members, entries = ids.shape
+    width = padded(slots * members * (entries - slots))
+    return pl.pallas_call(
+        functools.partial(legendre_kernel, slots),
+        out_shape=(
+            jax.ShapeDtypeStruct((width, L), bf16),
+            jax.ShapeDtypeStruct((2 * members * slots, NPHI), bf16),
+        ),
+        in_specs=[SMEM],
+        out_specs=(VMEM, VMEM),
+        scratch_shapes=[
+            pltpu.VMEM((STEPS, BLOCKS, width), f32),
+            pltpu.VMEM((STEPS, BLOCKS, width), f32),
+            pltpu.VMEM((BLOCKS, width), f32),
+            pltpu.VMEM((BLOCKS, width), f32),
+            pltpu.VMEM((BLOCKS, width), f32),
+            pltpu.VMEM((width // LANES, L, LANES), f32),
+        ],
+        compiler_params=pltpu.CompilerParams(vmem_limit_bytes=LIMIT),
+        cost_estimate=work(2.0),
+        name="legendre_stage",
+    )(ids)
+
+
+def projection_kernel(ids_ref, turned_ref, beam_ref, folded_ref, sums, woven):
+    slots, share, cycles, depth = sums.shape
     sums[...] = jnp.zeros_like(sums)
-    for t in reversed(range(pieces)):
+    for t in reversed(range(L // ROWS)):
         for s in range(slots):
 
-            @pl.when(needed(s, t))
+            @pl.when(ids_ref[0, s] < (t + 1) * ROWS)
             def _():
-                copy(s, t).wait()
-                lhs = turned[s * cycles : (s + 1) * cycles, t * ROWS : (t + 1) * ROWS]
+                lhs = turned_ref[s * cycles : (s + 1) * cycles, t * ROWS : (t + 1) * ROWS]
                 for c in range(share):
                     sums[s, c] += jnp.dot(
-                        lhs, held[s, c, t * ROWS : (t + 1) * ROWS, :], preferred_element_type=f32
+                        lhs,
+                        beam_ref[s, c, t * ROWS : (t + 1) * ROWS, :],
+                        preferred_element_type=f32,
                     )
 
     for s in range(slots):
@@ -281,46 +351,30 @@
             folded_ref[s, :, j * LANES : (j + 1) * LANES] = woven[s, j].astype(bf16)
 
 
-def projection(m_table, ids, beam):
+def projection(ids, turned, beam, cycles):
     slots, share, _, depth = beam.shape
-    members, entries = ids.shape
-    cycles = members * (entries - slots)
-    width = padded(slots * cycles)
-    every = members * slots
     return pl.pallas_call(
         projection_kernel,
-        out_shape=(
-            jax.ShapeDtypeStruct((slots, cycles * share, depth), bf16),
-            jax.ShapeDtypeStruct((2 * every, NPHI), bf16),
-        ),
-        in_specs=[SMEM, SMEM, HBM],
-        out_specs=(VMEM, VMEM),
+        out_shape=jax.ShapeDtypeStruct((slots, cycles * share, depth), bf16),
+        in_specs=[SMEM, VMEM, VMEM],
+        out_specs=VMEM,
         scratch_shapes=[
-            pltpu.VMEM((slots, share, L, depth), bf16),
-            pltpu.VMEM((STEPS, BLOCKS, width), f32),
-            pltpu.VMEM((STEPS, BLOCKS, width), f32),
-            pltpu.VMEM((BLOCKS, width), f32),
-            pltpu.VMEM((BLOCKS, width), f32),
-            pltpu.VMEM((BLOCKS, width), f32),
-            pltpu.VMEM((width // LANES, L, LANES), f32),
-            pltpu.VMEM((width, L), bf16),
             pltpu.VMEM((slots, share, cycles, depth), f32),
             pltpu.VMEM((slots, depth // LANES, cycles * share, LANES), f32),
-            pltpu.SemaphoreType.DMA((slots, L // ROWS)),
         ],
         compiler_params=pltpu.CompilerParams(vmem_limit_bytes=LIMIT),
+        cost_estimate=work(2.0),
         name="projection",
-    )(m_table, ids, beam)
-
-
-def cycle_kernel(parts_ref, folded_ref, out_ref):
-    members, rows, columns = out_ref.shape
+    )(ids, turned, beam)
+
+
+def cycle_kernel(held_ref, got_ref, folded_ref, *out_refs):
+    members = len(out_refs)
+    rows, columns = out_refs[0].shape
     slots = folded_ref.shape[0]
     per_slot = columns // slots
     share = per_slot // PARTS
-    total = parts_ref[0].astype(f32)
-    for i in range(1, parts_ref.shape[0]):
-        total = total + parts_ref[i].astype(f32)
+    total = held_ref[0] + got_ref[0].astype(f32)
     singular = total.reshape(columns, total.shape[-1]).astype(bf16)
     shape = (members * rows, columns)
     values = jnp.zeros(shape, f32)
@@ -333,24 +387,25 @@
     same = iota(shape, 0) % share == (iota(shape, 1) // PARTS) % share
     values = jnp.where(same, values, 0.0).astype(bf16)
     for a in range(members):
-        out_ref[a] = values[a * rows : (a + 1) * rows]
-
-
-def cycle_values(parts, folded, members):
-    _, slots, per_slot, _ = parts.shape
+        out_refs[a][...] = values[a * rows : (a + 1) * rows]
+
+
+def cycle_values(held, got, folded, members):
+    _, slots, per_slot, _ = held.shape
     rows = folded.shape[1] // members
     return pl.pallas_call(
         cycle_kernel,
-        out_shape=jax.ShapeDtypeStruct((members, rows, slots * per_slot), bf16),
-        in_specs=[VMEM, VMEM],
-        out_specs=VMEM,
+        out_shape=(jax.ShapeDtypeStruct((rows, slots * per_slot), bf16),) * members,
+        in_specs=[VMEM, VMEM, VMEM],
+        out_specs=(VMEM,) * members,
         compiler_params=pltpu.CompilerParams(vmem_limit_bytes=LIMIT),
         name="cycle_values",
-    )(parts, folded)
-
-
-def sky_kernel(values_ref, fourier_ref, out_ref):
-    members, rows, columns = values_ref.shape
+    )(held, got, folded)
+
+
+def sky_kernel(members, *refs):
+    values_refs, (fourier_ref, out_ref) = refs[:members], refs[members:]
+    rows, columns = values_refs[0].shape
     every = fourier_ref.shape[0] // 2
     slots = every // members
     per_slot = columns // slots
@@ -364,33 +419,50 @@
         for a in range(members):
             choose = (part // 2 == d) & (target == (part % 2) * every + a * slots + slot)
             folded = folded + jnp.dot(
-                values_ref[a], jnp.where(choose, 1.0, 0.0).astype(bf16), preferred_element_type=f32
+                values_refs[a][...], jnp.where(choose, 1.0, 0.0).astype(bf16), preferred_element_type=f32
             )
         maps = jnp.dot(folded.astype(bf16), fourier_ref[...], preferred_element_type=f32)
         out_ref[:, d] = maps.reshape(rows // share, share, NPHI)
 
 
 def sky_maps(values, fourier, share):
-    members, rows, columns = values.shape
-    return pl.pallas_call(
-        sky_kernel,
+    members = len(values)
+    rows = values[0].shape[0]
+    return pl.pallas_call(
+        functools.partial(sky_kernel, members),
         out_shape=jax.ShapeDtypeStruct((rows // share, 2, share, NPHI), f32),
-        in_specs=[VMEM, VMEM],
+        in_specs=[VMEM] * (members + 1),
         out_specs=VMEM,
         compiler_params=pltpu.CompilerParams(vmem_limit_bytes=LIMIT),
         name="sky_maps",
-    )(values, fourier)
+    )(*values, fourier)
+
+
+def swap(value, axis, size, bit):
+    return lax.ppermute(value, axis, [(k, k ^ bit) for k in range(size)])
 
 
 def local(members, pieces, m_table, retained_modes, cycle_ids, kl_coeffs, kl_vectors, beam_matrix):
-    ids = lax.all_gather(jnp.concatenate([m_table, cycle_ids]), "ma", axis=0, tiled=False)
-    offset = (lax.axis_index("freq") * kl_coeffs.shape[2]).astype(jnp.int32).reshape(1)
-    sums = kl_stage(offset, retained_modes, kl_coeffs, kl_vectors, pieces)
-    parts = lax.all_to_all(sums, "freq", split_axis=0, concat_axis=0, tiled=True)
-    folded, fourier = projection(m_table, ids, beam_matrix)
-    values = cycle_values(parts, folded, members)
-    values = lax.all_to_all(values, "ma", split_axis=0, concat_axis=0, tiled=True)
-    return sky_maps(values, fourier, beam_matrix.shape[1])
+    slots, share = beam_matrix.shape[:2]
+    ids = lead(jnp.concatenate([m_table, cycle_ids])[None])
+    bit = 1
+    while bit < members:
+        far = swap(ids, "ma", members, bit)
+        ids = stack(ids, far)
+        bit *= 2
+    held, send = kl_stage(retained_modes, kl_coeffs, kl_vectors, pieces)
+    bit = 1
+    while True:
+        got = swap(send, "freq", pieces, bit)
+        bit *= 2
+        if bit == pieces:
+            break
+        held, send = fold_stage(bit, held, got)
+    turned, fourier = legendre_stage(ids, slots)
+    folded = projection(ids, turned, beam_matrix, members * cycle_ids.shape[0])
+    values = cycle_values(held, got, folded, members)
+    values = [swap(x, "ma", members, j) if j else x for j, x in enumerate(values)]
+    return sky_maps(values, fourier, share)
 
 
 def solution(mesh):

time: 36.6 us -> 33.6 us (0.918)
  blocking collectives: 14.6 us -> 0 us
  starting transfers between devices: 6.37 us -> 14.3 us
  waiting for transfers between devices: 0.01 us -> 7.49 us
  local copies, waits for them, and re-layouts: 5.7 us -> 3.53 us
  Pallas kernels: 8.03 us -> 7.15 us
  between operations: 0.67 us -> 0.06 us
    ppermute x0 -> x8, starting transfers between devices: none -> 14.3 us  [swap(): return lax.ppermute(value, axis, [(k, k ^ bit) for k in range(size)])]
    ppermute x0 -> x8, waiting for transfers between devices: none -> 7.49 us  [swap(): return lax.ppermute(value, axis, [(k, k ^ bit) for k in range(size)])]
    unnamed x1 -> x0, blocking collectives: 7.37 us -> none
    all_to_all x1 -> x0, blocking collectives: 7.26 us -> none  [local(): lax.all_to_all(values, 'ma', split_axis=0, concat_axis=0, tiled=True)]
    all_to_all x1 -> x0, starting transfers between devices: 6.37 us -> none  [local(): lax.all_to_all(sums, 'freq', split_axis=0, concat_axis=0, tiled=True)]
    unnamed x12 -> x10, local copies, waits for them, and re-layouts: 5.62 us -> 3.53 us
    broadcast_in_dim x0 -> x1, other arithmetic: none -> 0.9 us  [local(): ids = lead(jnp.concatenate([m_table, cycle_ids])[None])]
    pallas_call x4 -> x10, Pallas kernels: 8.03 us -> 7.15 us  [the longest x1 2.11 us: projection(): pl.pallas_call(projection_kernel, out_shape=jax.ShapeDtypeStruct((slots,...]
  transfers between devices with their start and end apart: 1 -> 8, of which waited for: 0 -> 6; matrix products, arithmetic and copies ran while one was open for 6% -> 3% of each run, Pallas kernels for 10% -> 12%
where the time goes in v2:
time: 33.6 us; the launch traced here: 33.4 us
  starting transfers between devices  14.3 us (43%)
  waiting for transfers between devices  7.49 us (22%)
  Pallas kernels  7.15 us (21%)
  local copies, waits for them, and re-layouts  3.53 us (11%)
  other arithmetic  0.9 us (3%)
    ppermute x8, starting transfers between devices, swap(): return lax.ppermute(value, axis, [(k, k ^ bit) for k in range(size)])  14.3 us
    ppermute x8, waiting for transfers between devices, swap(): return lax.ppermute(value, axis, [(k, k ^ bit) for k in range(size)])  7.49 us
    unnamed x10, local copies, waits for them, and re-layouts  3.53 us
    pallas_call x1, Pallas kernels, projection(): pl.pallas_call(projection_kernel, out_shape=jax.ShapeDtypeStruct((slots,...  2.11 us
    pallas_call x1, Pallas kernels, legendre_stage(): pl.pallas_call(functools.partial(legendre_kernel, slots), out_shape=(jax....  1.93 us
    pallas_call x1, Pallas kernels, kl_stage(): pl.pallas_call(kl_kernel, out_shape=(jax.ShapeDtypeStruct(shape, f32), ja...  1.54 us
    pallas_call x1, Pallas kernels, sky_maps(): pl.pallas_call(functools.partial(sky_kernel, members), out_shape=jax.Shap...  1.3 us
    broadcast_in_dim x1, other arithmetic, local(): ids = lead(jnp.concatenate([m_table, cycle_ids])[None])  0.9 us
  transfers between devices with their start and end apart: 8, of which 6 were waited for; matrix products, arithmetic and copies ran while one was open for 3% of the time, Pallas kernels for 12%

profile of v2, /device:TPU:0, one launch (start us, length us, event | category | flops | bytes accessed | tf_op | source)
XLA Modules:
  0.0 33.4 jit_solution(15406740535702461264)
XLA Ops:
  0.0 0.0 copy-start
  0.0 2.2 %copy-done = bf16[2,64,32,512]{3,2,1,0:T(8,128)(2,1)S(1)} copy-done((bf16[2,64,32,512]{3,2,1,0:T(8,128)(2,1)S(1)}, bf16[2,64,32,512]{3,2,1,0:T(8,128)(2,1)}, u32[]{:S(2)}) %copy-start) | copy-done | bytes 4194328
  2.2 0.0 copy-start.1
  2.2 0.7 %copy-done.1 = bf16[2,4,64]{2,1,0:T(4,128)(2,1)S(1)} copy-done((bf16[2,4,64]{2,1,0:T(4,128)(2,1)S(1)}, bf16[2,4,64]{2,1,0:T(4,128)(2,1)}, u32[]{:S(2)}) %copy-start.1) | copy-done | bytes 1048
  2.9 0.0 copy-start.2
  2.9 0.7 %copy-done.2 = s32[2]{0:T(128)S(1)} copy-done((s32[2]{0:T(128)S(1)}, s32[2]{0:T(128)}, u32[]{:S(2)}) %copy-start.2) | copy-done | bytes 32
  3.5 1.5 %kl_stage.1 = (f32[4,2,16,512]{3,2,1,0:T(8,128)S(1)}, bf16[4,2,16,512]{3,2,1,0:T(8,128)(2,1)S(1)}) custom-call(s32[2]{0:T(128)S(1)} %copy-done.2, bf16[2,4,64]{2,1,0:T(4,128)(2,1)S(1)} %copy-done.1, bf16[2,64,32,512]{3,2,1,0:T(8,128)(2,1)S(1)} %copy-done), custom_call_target="tpu_custom_call" | custom-call | flops 2000000000 | bytes 4096 | tf_op jit(solution)/shard_map/kl_stage/pallas_call | solution.py:79
  5.1 0.6 %collective-permute-start = (bf16[4,2,16,512]{3,2,1,0:T(8,128)(2,1)S(1)}, bf16[4,2,16,512]{3,2,1,0:T(8,128)(2,1)S(1)}, u32[]{:S(2)}, u32[]{:S(2)}) collective-permute-start(bf16[4,2,16,512]{3,2,1,0:T(8,128)(2,1)S(1)} %get-tuple-element.18), channel_id=1, source_target_pairs={{0,1},{1,0},{2,3},{3,2},{4,5},{5,4},{6,7},{7,6},{8,9},{9,8},{10,11... | collective-permute-start | bytes 393224 | tf_op jit(solution)/shard_map/ppermute | solution.py:442
  5.6 0.0 slice-start
  5.6 0.9 %add_bitcast_fusion.in_ref = s32[1,10]{1,0:T(1,128)S(1)} fusion(s32[8]{0:T(128)} %param.8, s32[2]{0:T(128)} %param.6), kind=kLoop, calls=%fused_computation | loop fusion | flops 10 | bytes 80 | tf_op jit(solution)/shard_map/broadcast_in_dim | solution.py:447
  6.5 0.0 slice-start.1
  6.5 2.5 %collective-permute-start.3 = (s32[1,10]{1,0:T(1,128)S(1)}, s32[1,10]{1,0:T(1,128)S(1)}, u32[]{:S(2)}, u32[]{:S(2)}) collective-permute-start(s32[1,10]{1,0:T(1,128)S(1)} %lead.1.low_ref), channel_id=1, source_target_pairs={{0,8},{8,0},{16,24},{24,16},{1,9},{9,1},{17,25},{25,17},{2,10},{10... | collective-permute-start | bytes 128 | tf_op jit(solution)/shard_map/ppermute | solution.py:442
  9.0 1.5 %collective-permute-done.3.high_ref = s32[1,10]{1,0:T(1,128)S(1)} collective-permute-done((s32[1,10]{1,0:T(1,128)S(1)}, s32[1,10]{1,0:T(1,128)S(1)}, u32[]{:S(2)}, u32[]{:S(2)}) %collective-permute-start.3) | collective-permute-done | bytes 72 | tf_op jit(solution)/shard_map/ppermute | solution.py:442
  10.6 2.0 %collective-permute-start.4 = (s32[2,10]{1,0:T(2,128)S(1)}, s32[2,10]{1,0:T(2,128)S(1)}, u32[]{:S(2)}, u32[]{:S(2)}) collective-permute-start(s32[2,10]{1,0:T(2,128)S(1)} %stack.2.low_ref), channel_id=1, source_target_pairs={{0,16},{8,24},{16,0},{24,8},{1,17},{9,25},{17,1},{25,9},{2,18},{10... | collective-permute-start | bytes 248 | tf_op jit(solution)/shard_map/ppermute | solution.py:442
  12.6 1.6 %collective-permute-done.4.high_ref = s32[2,10]{1,0:T(2,128)S(1)} collective-permute-done((s32[2,10]{1,0:T(2,128)S(1)}, s32[2,10]{1,0:T(2,128)S(1)}, u32[]{:S(2)}, u32[]{:S(2)}) %collective-permute-start.4) | collective-permute-done | bytes 112 | tf_op jit(solution)/shard_map/ppermute | solution.py:442
  14.2 0.0 collective-permute-done.got_ref
  14.2 2.1 %collective-permute-start.1 = (bf16[2,2,16,512]{3,2,1,0:T(8,128)(2,1)S(1)}, bf16[2,2,16,512]{3,2,1,0:T(8,128)(2,1)S(1)}, u32[]{:S(2)}, u32[]{:S(2)}) collective-permute-start(bf16[2,2,16,512]{3,2,1,0:T(8,128)(2,1)S(1)} %get-tuple-element.20), channel_id=1, source_target_pairs={{0,2},{1,3},{2,0},{3,1},{4,6},{5,7},{6,4},{7,5},{8,10},{9,11},{10,... | collective-permute-start | bytes 196616 | tf_op jit(solution)/shard_map/ppermute | solution.py:442
  16.4 1.9 %legendre_stage.1 = (bf16[128,1024]{1,0:T(8,128)(2,1)S(1)}, bf16[16,2048]{1,0:T(8,128)(2,1)S(1)}) custom-call(s32[4,10]{1,0:T(4,128)S(1)} %stack.3.ids_ref), custom_call_target="tpu_custom_call" | custom-call | flops 2000000000 | bytes 4096 | tf_op jit(solution)/shard_map/legendre_stage/pallas_call | solution.py:306
  18.3 0.3 collective-permute-done.1.got_ref
  18.7 3.5 %collective-permute-start.2 = (bf16[1,2,16,512]{3,2,1,0:T(8,128)(2,1)S(1)}, bf16[1,2,16,512]{3,2,1,0:T(8,128)(2,1)S(1)}, u32[]{:S(2)}, u32[]{:S(2)}) collective-permute-start(bf16[1,2,16,512]{3,2,1,0:T(8,128)(2,1)S(1)} %get-tuple-element.22), channel_id=1, source_target_pairs={{0,4},{1,5},{2,6},{3,7},{4,0},{5,1},{6,2},{7,3},{8,12},{9,13},{10,... | collective-permute-start | bytes 98312 | tf_op jit(solution)/shard_map/ppermute | solution.py:442
  22.1 0.0 slice-done
  22.1 0.0 slice-done.1
  22.1 2.1 %projection.1.folded_ref = bf16[2,128,512]{2,1,0:T(8,128)(2,1)S(1)} custom-call(s32[4,10]{1,0:T(4,128)S(1)} %stack.3.ids_ref, bf16[128,1024]{1,0:T(8,128)(2,1)S(1)} %get-tuple-element.23.turned_ref, bf16[2,4,1024,512]{3,2,1,0:T(8,128)(2,1)S(1)} %bitcast.3), custom_call_target="tpu_custom_call" | custom-call | flops 2000000000 | bytes 4096 | tf_op jit(solution)/shard_map/projection/pallas_call | solution.py:356
  24.2 0.0 collective-permute-done.2.got_ref
  24.2 0.2 cycle_values.1
  24.5 1.6 %collective-permute-start.5 = (bf16[32,32]{1,0:T(8,128)(2,1)S(1)}, bf16[32,32]{1,0:T(8,128)(2,1)S(1)}, u32[]{:S(2)}, u32[]{:S(2)}) collective-permute-start(bf16[32,32]{1,0:T(8,128)(2,1)S(1)} %get-tuple-element.25), channel_id=1, source_target_pairs={{0,8},{8,0},{16,24},{24,16},{1,9},{9,1},{17,25},{25,17},{2,10},{10... | collective-permute-start | bytes 6152 | tf_op jit(solution)/shard_map/ppermute | solution.py:442
  26.0 1.5 %collective-permute-start.6 = (bf16[32,32]{1,0:T(8,128)(2,1)S(1)}, bf16[32,32]{1,0:T(8,128)(2,1)S(1)}, u32[]{:S(2)}, u32[]{:S(2)}) collective-permute-start(bf16[32,32]{1,0:T(8,128)(2,1)S(1)} %get-tuple-element.26), channel_id=1, source_target_pairs={{0,16},{8,24},{16,0},{24,8},{1,17},{9,25},{17,1},{25,9},{2,18},{10... | collective-permute-start | bytes 6152 | tf_op jit(solution)/shard_map/ppermute | solution.py:442
  27.5 0.5 %collective-permute-start.7 = (bf16[32,32]{1,0:T(8,128)(2,1)S(1)}, bf16[32,32]{1,0:T(8,128)(2,1)S(1)}, u32[]{:S(2)}, u32[]{:S(2)}) collective-permute-start(bf16[32,32]{1,0:T(8,128)(2,1)S(1)} %get-tuple-element.27), channel_id=1, source_target_pairs={{0,24},{8,16},{16,8},{24,0},{1,25},{9,17},{17,9},{25,1},{2,26},{10... | collective-permute-start | bytes 6152 | tf_op jit(solution)/shard_map/ppermute | solution.py:442
  28.0 0.2 collective-permute-done.5.refs_1_
  28.2 1.5 %collective-permute-done.6.refs_2_ = bf16[32,32]{1,0:T(8,128)(2,1)S(1)} collective-permute-done((bf16[32,32]{1,0:T(8,128)(2,1)S(1)}, bf16[32,32]{1,0:T(8,128)(2,1)S(1)}, u32[]{:S(2)}, u32[]{:S(2)}) %collective-permute-start.6) | collective-permute-done | bytes 2080 | tf_op jit(solution)/shard_map/ppermute | solution.py:442
  29.7 2.4 %collective-permute-done.7.refs_3_ = bf16[32,32]{1,0:T(8,128)(2,1)S(1)} collective-permute-done((bf16[32,32]{1,0:T(8,128)(2,1)S(1)}, bf16[32,32]{1,0:T(8,128)(2,1)S(1)}, u32[]{:S(2)}, u32[]{:S(2)}) %collective-permute-start.7) | collective-permute-done | bytes 2080 | tf_op jit(solution)/shard_map/ppermute | solution.py:442
  32.1 1.3 %sky_maps.1 = f32[8,2,4,2048]{3,2,1,0:T(4,128)} custom-call(bf16[32,32]{1,0:T(8,128)(2,1)S(1)} %get-tuple-element.24.refs_0_, bf16[32,32]{1,0:T(8,128)(2,1)S(1)} %collective-permute-done.5.refs_1_, bf16[32,32]{1,0:T(8,128)(2,1)S(1)} %collective-permute-done.6.refs_2_, bf16[32,32]{1,0:T(8,128)(2,1)S(1)} %collective-permute-done.7.refs_3_, ...), custom_call_target="tpu_custom_call" | custom-call | tf_op jit(solution)/shard_map/sky_maps/pallas_call | solution.py:431
  (6 shorter events, 0.1 us)
Async XLA Ops:
  0.0 2.2 %copy-start = (bf16[2,64,32,512]{3,2,1,0:T(8,128)(2,1)S(1)}, bf16[2,64,32,512]{3,2,1,0:T(8,128)(2,1)}, u32[]{:S(2)}) copy-start(bf16[2,64,32,512]{3,2,1,0:T(8,128)(2,1)} %vectors_ref.1) | copy-start | bytes 12582916
  2.2 0.7 %copy-start.1 = (bf16[2,4,64]{2,1,0:T(4,128)(2,1)S(1)}, bf16[2,4,64]{2,1,0:T(4,128)(2,1)}, u32[]{:S(2)}) copy-start(bf16[2,4,64]{2,1,0:T(4,128)(2,1)} %coeff_ref.1) | copy-start | bytes 3076
  2.9 0.7 %copy-start.2 = (s32[2]{0:T(128)S(1)}, s32[2]{0:T(128)}, u32[]{:S(2)}) copy-start(s32[2]{0:T(128)} %kept_ref.1) | copy-start | bytes 28
  5.1 9.1 %collective-permute-start = (bf16[4,2,16,512]{3,2,1,0:T(8,128)(2,1)S(1)}, bf16[4,2,16,512]{3,2,1,0:T(8,128)(2,1)S(1)}, u32[]{:S(2)}, u32[]{:S(2)}) collective-permute-start(bf16[4,2,16,512]{3,2,1,0:T(8,128)(2,1)S(1)} %get-tuple-element.18), channel_id=1, source_target_pairs={{0,1},{1,0},{2,3},{3,2},{4,5},{5,4},{6,7},{7,6},{8,9},{9,8},{10,11... | collective-permute-start | bytes 393224 | tf_op jit(solution)/shard_map/ppermute | solution.py:442
  5.6 16.5 %slice-start = ((s8[8388608]{0:T(1024)(128)(4,1)}), s8[4194304]{0:T(1024)(128)(4,1)S(1)}, s32[]{:S(2)}) async-start(s8[8388608]{0:T(1024)(128)(4,1)} %bitcast.2), calls=%async_computation | async-start | bytes 8388608
  6.5 15.6 %slice-start.1 = ((s8[8388608]{0:T(1024)(128)(4,1)}), s8[4194304]{0:T(1024)(128)(4,1)S(1)}, s32[]{:S(2)}) async-start(s8[8388608]{0:T(1024)(128)(4,1)} %bitcast.2), calls=%async_computation.1 | async-start | bytes 8388608
  6.5 4.1 %collective-permute-start.3 = (s32[1,10]{1,0:T(1,128)S(1)}, s32[1,10]{1,0:T(1,128)S(1)}, u32[]{:S(2)}, u32[]{:S(2)}) collective-permute-start(s32[1,10]{1,0:T(1,128)S(1)} %lead.1.low_ref), channel_id=1, source_target_pairs={{0,8},{8,0},{16,24},{24,16},{1,9},{9,1},{17,25},{25,17},{2,10},{10... | collective-permute-start | bytes 128 | tf_op jit(solution)/shard_map/ppermute | solution.py:442
  10.6 3.6 %collective-permute-start.4 = (s32[2,10]{1,0:T(2,128)S(1)}, s32[2,10]{1,0:T(2,128)S(1)}, u32[]{:S(2)}, u32[]{:S(2)}) collective-permute-start(s32[2,10]{1,0:T(2,128)S(1)} %stack.2.low_ref), channel_id=1, source_target_pairs={{0,16},{8,24},{16,0},{24,8},{1,17},{9,25},{17,1},{25,9},{2,18},{10... | collective-permute-start | bytes 248 | tf_op jit(solution)/shard_map/ppermute | solution.py:442
  14.2 4.4 %collective-permute-start.1 = (bf16[2,2,16,512]{3,2,1,0:T(8,128)(2,1)S(1)}, bf16[2,2,16,512]{3,2,1,0:T(8,128)(2,1)S(1)}, u32[]{:S(2)}, u32[]{:S(2)}) collective-permute-start(bf16[2,2,16,512]{3,2,1,0:T(8,128)(2,1)S(1)} %get-tuple-element.20), channel_id=1, source_target_pairs={{0,2},{1,3},{2,0},{3,1},{4,6},{5,7},{6,4},{7,5},{8,10},{9,11},{10,... | collective-permute-start | bytes 196616 | tf_op jit(solution)/shard_map/ppermute | solution.py:442
  18.7 5.6 %collective-permute-start.2 = (bf16[1,2,16,512]{3,2,1,0:T(8,128)(2,1)S(1)}, bf16[1,2,16,512]{3,2,1,0:T(8,128)(2,1)S(1)}, u32[]{:S(2)}, u32[]{:S(2)}) collective-permute-start(bf16[1,2,16,512]{3,2,1,0:T(8,128)(2,1)S(1)} %get-tuple-element.22), channel_id=1, source_target_pairs={{0,4},{1,5},{2,6},{3,7},{4,0},{5,1},{6,2},{7,3},{8,12},{9,13},{10,... | collective-permute-start | bytes 98312 | tf_op jit(solution)/shard_map/ppermute | solution.py:442
  24.5 3.7 %collective-permute-start.5 = (bf16[32,32]{1,0:T(8,128)(2,1)S(1)}, bf16[32,32]{1,0:T(8,128)(2,1)S(1)}, u32[]{:S(2)}, u32[]{:S(2)}) collective-permute-start(bf16[32,32]{1,0:T(8,128)(2,1)S(1)} %get-tuple-element.25), channel_id=1, source_target_pairs={{0,8},{8,0},{16,24},{24,16},{1,9},{9,1},{17,25},{25,17},{2,10},{10... | collective-permute-start | bytes 6152 | tf_op jit(solution)/shard_map/ppermute | solution.py:442
  26.0 3.7 %collective-permute-start.6 = (bf16[32,32]{1,0:T(8,128)(2,1)S(1)}, bf16[32,32]{1,0:T(8,128)(2,1)S(1)}, u32[]{:S(2)}, u32[]{:S(2)}) collective-permute-start(bf16[32,32]{1,0:T(8,128)(2,1)S(1)} %get-tuple-element.26), channel_id=1, source_target_pairs={{0,16},{8,24},{16,0},{24,8},{1,17},{9,25},{17,1},{25,9},{2,18},{10... | collective-permute-start | bytes 6152 | tf_op jit(solution)/shard_map/ppermute | solution.py:442
  27.5 4.5 %collective-permute-start.7 = (bf16[32,32]{1,0:T(8,128)(2,1)S(1)}, bf16[32,32]{1,0:T(8,128)(2,1)S(1)}, u32[]{:S(2)}, u32[]{:S(2)}) collective-permute-start(bf16[32,32]{1,0:T(8,128)(2,1)S(1)} %get-tuple-element.27), channel_id=1, source_target_pairs={{0,24},{8,16},{16,8},{24,0},{1,25},{9,17},{17,9},{25,1},{2,26},{10... | collective-permute-start | bytes 6152 | tf_op jit(solution)/shard_map/ppermute | solution.py:442

commit v3 on v2

--- a/solution.py
+++ b/solution.py
@@ -17,6 +17,7 @@
 STEPS = L // BLOCKS
 ROWS = 256
 LANES = 128
+CHUNKS = 4
 GROUP = 16
 
 
@@ -43,26 +44,71 @@
     )
 
 
-def kl_kernel(kept_ref, coeff_ref, vectors_ref, keep_ref, send_ref, spread, ready):
+def lead_kernel(in_ref, out_ref):
+    out_ref[...] = in_ref[...]
+
+
+def lead(ids):
+    return pl.pallas_call(
+        lead_kernel,
+        out_shape=jax.ShapeDtypeStruct(ids.shape, ids.dtype),
+        in_specs=[VMEM],
+        out_specs=VMEM,
+        compiler_params=pltpu.CompilerParams(vmem_limit_bytes=SMALL),
+        cost_estimate=work(4.0),
+        name="lead",
+    )(ids)
+
+
+def spread_kernel(kept_ref, coeff_ref, out_ref):
+    slots, rows, columns = out_ref.shape
+    modes = coeff_ref.shape[2]
+    group = columns // modes
+    place = lax.axis_index("freq")
+    expand = (iota((modes, columns), 1) // group == iota((modes, columns), 0)).astype(bf16)
+    mode_index = place * modes + iota((PARTS, modes), 1)
+    tall = []
+    for s in range(slots):
+        masked = jnp.where(mode_index < kept_ref[s], coeff_ref[s].astype(f32), 0.0)
+        tall += [masked] * group
+    wide = jnp.dot(
+        jnp.concatenate(tall, axis=0).astype(bf16), expand, preferred_element_type=f32
+    )
+    period = max(group, LANES)
+    diagonal = iota((rows, period), 1) % group == iota((rows, period), 0) // PARTS
+    for s in range(slots):
+        for t in range(columns // period):
+            lanes = slice(t * period, (t + 1) * period)
+            piece = wide[s * rows : (s + 1) * rows, lanes]
+            out_ref[s, :, lanes] = jnp.where(diagonal, piece, 0.0).astype(bf16)
+
+
+def spread_stage(kept, coeffs, channels):
+    slots, _, modes = coeffs.shape
+    group = min(GROUP, channels)
+    return pl.pallas_call(
+        spread_kernel,
+        out_shape=jax.ShapeDtypeStruct((slots, group * PARTS, modes * group), bf16),
+        in_specs=[SMEM, VMEM],
+        out_specs=VMEM,
+        compiler_params=pltpu.CompilerParams(vmem_limit_bytes=SMALL),
+        cost_estimate=work(1.0),
+        name="spread_stage",
+    )(kept, coeffs)
+
+
+def kl_kernel(spread_ref, vectors_ref, keep_ref, send_ref, ready):
     slots, modes, channels, depth = vectors_ref.shape
-    group = min(GROUP, channels)
+    group = spread_ref.shape[1] // PARTS
     pieces = keep_ref.shape[0] * 2
     share = channels // pieces
-    place = lax.axis_index("freq")
-    rows, columns = group * PARTS, modes * group
-    expand = (iota((modes, columns), 1) // group == iota((modes, columns), 0)).astype(bf16)
-    mode_index = place * modes + iota((PARTS, modes), 1)
-    diagonal = iota((rows, columns), 1) % group == iota((rows, columns), 0) // PARTS
-    for s in range(slots):
-        masked = jnp.where(mode_index < kept_ref[s], coeff_ref[s].astype(f32), 0.0)
-        tall = jnp.concatenate([masked] * group, axis=0).astype(bf16)
-        wide = jnp.dot(tall, expand, preferred_element_type=f32)
-        spread[s] = jnp.where(diagonal, wide, 0.0).astype(bf16)
-    parity = place % 2
+    parity = lax.axis_index("freq") % 2
     for s in range(slots):
         for g in range(channels // group):
-            block = vectors_ref[s, :, g * group : (g + 1) * group, :].reshape(columns, depth)
-            sums = jnp.dot(spread[s], block, preferred_element_type=f32)
+            block = vectors_ref[s, :, g * group : (g + 1) * group, :]
+            sums = jnp.dot(
+                spread_ref[s], block.reshape(modes * group, depth), preferred_element_type=f32
+            )
             for i in range(group // share):
                 piece = g * (group // share) + i
                 ready[(piece + parity) % 2, piece // 2, s] = sums[
@@ -72,23 +118,19 @@
     send_ref[...] = ready[1].astype(bf16)
 
 
-def kl_stage(kept, coeffs, vectors, pieces):
-    slots, modes, channels, depth = vectors.shape
-    group = min(GROUP, channels)
+def kl_stage(spread, vectors, pieces):
+    slots, _, channels, depth = vectors.shape
     shape = (pieces // 2, slots, channels // pieces * PARTS, depth)
     return pl.pallas_call(
         kl_kernel,
         out_shape=(jax.ShapeDtypeStruct(shape, f32), jax.ShapeDtypeStruct(shape, bf16)),
-        in_specs=[SMEM, VMEM, VMEM],
+        in_specs=[VMEM, VMEM],
         out_specs=(VMEM, VMEM),
-        scratch_shapes=[
-            pltpu.VMEM((slots, group * PARTS, modes * group), bf16),
-            pltpu.VMEM((2, *shape), f32),
-        ],
+        scratch_shapes=[pltpu.VMEM((2, *shape), f32)],
         compiler_params=pltpu.CompilerParams(vmem_limit_bytes=LIMIT),
         cost_estimate=work(2.0),
         name="kl_stage",
-    )(kept, coeffs, vectors)
+    )(spread, vectors)
 
 
 def fold_kernel(bit, held_ref, got_ref, keep_ref, send_ref):
@@ -115,22 +157,6 @@
     rows = low_ref.shape[0]
     out_ref[:rows] = low_ref[...]
     out_ref[rows:] = high_ref[...]
-
-
-def copy_kernel(in_ref, out_ref):
-    out_ref[...] = in_ref[...]
-
-
-def lead(value):
-    return pl.pallas_call(
-        copy_kernel,
-        out_shape=jax.ShapeDtypeStruct(value.shape, value.dtype),
-        in_specs=[VMEM],
-        out_specs=VMEM,
-        compiler_params=pltpu.CompilerParams(vmem_limit_bytes=SMALL),
-        cost_estimate=work(4.0),
-        name="lead",
-    )(value)
 
 
 def stack(low, high):
@@ -270,7 +296,7 @@
 
 
 def legendre_kernel(
-    slots, ids_ref, turned_ref, fourier_ref, p_ref, q_ref, left, right, scale, table
+    slots, per_slot, ids_ref, turned_ref, fourier_ref, p_ref, q_ref, left, right, scale, table
 ):
     members, entries = ids_ref.shape
     cycles_each = entries - slots
@@ -296,18 +322,20 @@
         for s in range(slots):
             m_every = jnp.where(row == a * slots + s, ids_ref[a, s], m_every)
     real, imaginary = fourier_rows(m_every)
-    fourier_ref[:every] = real.astype(bf16)
-    fourier_ref[every:] = imaginary.astype(bf16)
-
-
-def legendre_stage(ids, slots):
+    is_real = iota((per_slot, NPHI), 0) % 2 == 0
+    for j in range(every):
+        rows = jnp.where(is_real, real[j : j + 1], imaginary[j : j + 1])
+        fourier_ref[j * per_slot : (j + 1) * per_slot] = rows.astype(bf16)
+
+
+def legendre_stage(ids, slots, per_slot):
     members, entries = ids.shape
     width = padded(slots * members * (entries - slots))
     return pl.pallas_call(
-        functools.partial(legendre_kernel, slots),
+        functools.partial(legendre_kernel, slots, per_slot),
         out_shape=(
             jax.ShapeDtypeStruct((width, L), bf16),
-            jax.ShapeDtypeStruct((2 * members * slots, NPHI), bf16),
+            jax.ShapeDtypeStruct((members * slots * per_slot, NPHI), bf16),
         ),
         in_specs=[SMEM],
         out_specs=(VMEM, VMEM),
@@ -372,19 +400,22 @@
     members = len(out_refs)
     rows, columns = out_refs[0].shape
     slots = folded_ref.shape[0]
-    per_slot = columns // slots
+    per_member = columns // members
+    per_slot = per_member // slots
     share = per_slot // PARTS
     total = held_ref[0] + got_ref[0].astype(f32)
-    singular = total.reshape(columns, total.shape[-1]).astype(bf16)
+    singular = total.reshape(per_member, total.shape[-1]).astype(bf16)
+    singular = jnp.concatenate([singular] * members, axis=0)
     shape = (members * rows, columns)
+    row, column = iota(shape, 0), iota(shape, 1)
+    slot = (column // per_slot) % slots
     values = jnp.zeros(shape, f32)
     for s in range(slots):
         product = lax.dot_general(
-            folded_ref[s], singular, (((1,), (1,)), ((), ())),
-            preferred_element_type=f32,
+            folded_ref[s], singular, (((1,), (1,)), ((), ())), preferred_element_type=f32
         )
-        values = jnp.where(iota(shape, 1) // per_slot == s, product, values)
-    same = iota(shape, 0) % share == (iota(shape, 1) // PARTS) % share
+        values = jnp.where(slot == s, product, values)
+    same = (row % share == (column // PARTS) % share) & (row // rows == column // per_member)
     values = jnp.where(same, values, 0.0).astype(bf16)
     for a in range(members):
         out_refs[a][...] = values[a * rows : (a + 1) * rows]
@@ -393,9 +424,10 @@
 def cycle_values(held, got, folded, members):
     _, slots, per_slot, _ = held.shape
     rows = folded.shape[1] // members
+    shape = jax.ShapeDtypeStruct((rows, members * slots * per_slot), bf16)
     return pl.pallas_call(
         cycle_kernel,
-        out_shape=(jax.ShapeDtypeStruct((rows, slots * per_slot), bf16),) * members,
+        out_shape=(shape,) * members,
         in_specs=[VMEM, VMEM, VMEM],
         out_specs=(VMEM,) * members,
         compiler_params=pltpu.CompilerParams(vmem_limit_bytes=LIMIT),
@@ -404,35 +436,41 @@
 
 
 def sky_kernel(members, *refs):
-    values_refs, (fourier_ref, out_ref) = refs[:members], refs[members:]
+    values_refs, (fourier_ref, out_hbm, maps, sems) = refs[:members], refs[members:]
     rows, columns = values_refs[0].shape
-    every = fourier_ref.shape[0] // 2
-    slots = every // members
-    per_slot = columns // slots
-    share = per_slot // PARTS
-    shape = (columns, 2 * every)
-    part = iota(shape, 0) % PARTS
-    slot = iota(shape, 0) // per_slot
-    target = iota(shape, 1)
-    for d in range(2):
-        folded = jnp.zeros((rows, 2 * every), f32)
-        for a in range(members):
-            choose = (part // 2 == d) & (target == (part % 2) * every + a * slots + slot)
-            folded = folded + jnp.dot(
-                values_refs[a][...], jnp.where(choose, 1.0, 0.0).astype(bf16), preferred_element_type=f32
+    share = out_hbm.shape[2]
+    values = values_refs[0][...].astype(f32)
+    for ref in values_refs[1:]:
+        values = values + ref[...].astype(f32)
+    split = (iota((rows, columns), 1) % PARTS) // 2
+    both = jnp.concatenate([jnp.where(split == d, values, 0.0) for d in range(2)], axis=0)
+    both = both.astype(bf16)
+    width = NPHI // CHUNKS
+    copies = []
+    for t in range(CHUNKS):
+        part = slice(t * width, (t + 1) * width)
+        result = jnp.dot(both, fourier_ref[:, part], preferred_element_type=f32)
+        for d in range(2):
+            maps[:, d, :, part] = result[d * rows : (d + 1) * rows].reshape(
+                rows // share, share, width
             )
-        maps = jnp.dot(folded.astype(bf16), fourier_ref[...], preferred_element_type=f32)
-        out_ref[:, d] = maps.reshape(rows // share, share, NPHI)
+        copies.append(
+            pltpu.make_async_copy(maps.at[:, :, :, part], out_hbm.at[:, :, :, part], sems.at[t])
+        )
+        copies[-1].start()
+    for copy in copies:
+        copy.wait()
 
 
 def sky_maps(values, fourier, share):
     members = len(values)
-    rows = values[0].shape[0]
+    shape = (values[0].shape[0] // share, 2, share, NPHI)
     return pl.pallas_call(
         functools.partial(sky_kernel, members),
-        out_shape=jax.ShapeDtypeStruct((rows // share, 2, share, NPHI), f32),
+        out_shape=jax.ShapeDtypeStruct(shape, f32),
         in_specs=[VMEM] * (members + 1),
-        out_specs=VMEM,
+        out_specs=HBM,
+        scratch_shapes=[pltpu.VMEM(shape, f32), pltpu.SemaphoreType.DMA((CHUNKS,))],
         compiler_params=pltpu.CompilerParams(vmem_limit_bytes=LIMIT),
         name="sky_maps",
     )(*values, fourier)
@@ -450,7 +488,8 @@
         far = swap(ids, "ma", members, bit)
         ids = stack(ids, far)
         bit *= 2
-    held, send = kl_stage(retained_modes, kl_coeffs, kl_vectors, pieces)
+    spread = spread_stage(retained_modes, kl_coeffs, kl_vectors.shape[2])
+    held, send = kl_stage(spread, kl_vectors, pieces)
     bit = 1
     while True:
         got = swap(send, "freq", pieces, bit)
@@ -458,10 +497,13 @@
         if bit == pieces:
             break
         held, send = fold_stage(bit, held, got)
-    turned, fourier = legendre_stage(ids, slots)
+    turned, fourier = legendre_stage(ids, slots, share * PARTS)
     folded = projection(ids, turned, beam_matrix, members * cycle_ids.shape[0])
     values = cycle_values(held, got, folded, members)
-    values = [swap(x, "ma", members, j) if j else x for j, x in enumerate(values)]
+    gathered = [values[0]]
+    for j in range(1, members):
+        gathered.append(swap(values[j], "ma", members, j))
+    values = gathered
     return sky_maps(values, fourier, share)
 
 

time: 33.6 us -> 32.5 us (0.967)
  other arithmetic: 0.9 us -> 0.08 us
    pallas_call x3 -> x4, Pallas kernels: 2.14 us -> 3.04 us  [the longest x1 2.06 us: legendre_stage(): pl.pallas_call(functools.partial(legendre_kernel, slots, per_slot), out_s...]
    broadcast_in_dim x1, other arithmetic: 0.9 us -> 0.07 us  [local(): ids = lead(jnp.concatenate([m_table, cycle_ids])[None])]
    pallas_call x1, Pallas kernels: 1.54 us -> 0.85 us  [kl_stage(): pl.pallas_call(kl_kernel, out_shape=(jax.ShapeDtypeStruct(shape, f32), ja...]
    unnamed x10 -> x14, local copies, waits for them, and re-layouts: 3.53 us -> 3.53 us
  transfers between devices with their start and end apart: 8 -> 8, of which waited for: 6 -> 6; matrix products, arithmetic and copies ran while one was open for 3% -> 0% of each run, Pallas kernels for 12% -> 13%
where the time goes in v3:
time: 32.5 us; the launch traced here: 32.4 us
  starting transfers between devices  14.3 us (44%)
  waiting for transfers between devices  7.35 us (23%)
  Pallas kernels  7.04 us (22%)
  local copies, waits for them, and re-layouts  3.53 us (11%)
    ppermute x8, starting transfers between devices, swap(): return lax.ppermute(value, axis, [(k, k ^ bit) for k in range(size)])  14.3 us
    ppermute x8, waiting for transfers between devices, swap(): return lax.ppermute(value, axis, [(k, k ^ bit) for k in range(size)])  7.35 us
    unnamed x14, local copies, waits for them, and re-layouts  3.53 us
    pallas_call x1, Pallas kernels, projection(): pl.pallas_call(projection_kernel, out_shape=jax.ShapeDtypeStruct((slots,...  2.11 us
    pallas_call x1, Pallas kernels, legendre_stage(): pl.pallas_call(functools.partial(legendre_kernel, slots, per_slot), out_s...  2.06 us
    pallas_call x1, Pallas kernels, sky_maps(): pl.pallas_call(functools.partial(sky_kernel, members), out_shape=jax.Shap...  0.98 us
    pallas_call x1, Pallas kernels, kl_stage(): pl.pallas_call(kl_kernel, out_shape=(jax.ShapeDtypeStruct(shape, f32), ja...  0.85 us
    pallas_call x1, Pallas kernels, spread_stage(): pl.pallas_call(spread_kernel, out_shape=jax.ShapeDtypeStruct((slots, grou...  0.75 us
  transfers between devices with their start and end apart: 8, of which 6 were waited for; matrix products, arithmetic and copies ran while one was open for 0% of the time, Pallas kernels for 13%

profile of v3, /device:TPU:0, one launch (start us, length us, event | category | flops | bytes accessed | tf_op | source)
XLA Modules:
  0.0 32.4 jit_solution(13392630419802891305)
XLA Ops:
  0.0 0.0 copy-start.1
  0.0 0.7 %copy-done.1 = bf16[2,4,64]{2,1,0:T(4,128)(2,1)S(1)} copy-done((bf16[2,4,64]{2,1,0:T(4,128)(2,1)S(1)}, bf16[2,4,64]{2,1,0:T(4,128)(2,1)}, u32[]{:S(2)}) %copy-start.1) | copy-done | bytes 1048
  0.7 0.7 %copy-done.2 = s32[2]{0:T(128)S(1)} copy-done((s32[2]{0:T(128)S(1)}, s32[2]{0:T(128)}, u32[]{:S(2)}) %copy-start.2) | copy-done | bytes 32
  1.3 0.7 %spread_stage.1.spread_ref = bf16[2,64,1024]{2,1,0:T(8,128)(2,1)S(1)} custom-call(s32[2]{0:T(128)S(1)} %copy-done.2, bf16[2,4,64]{2,1,0:T(4,128)(2,1)S(1)} %copy-done.1), custom_call_target="tpu_custom_call" | custom-call | flops 1000000000 | bytes 4096 | tf_op jit(solution)/shard_map/spread_stage/pallas_call | solution.py:89
  2.1 0.0 copy-start
  2.1 2.2 %copy-done = bf16[2,64,32,512]{3,2,1,0:T(8,128)(2,1)S(1)} copy-done((bf16[2,64,32,512]{3,2,1,0:T(8,128)(2,1)S(1)}, bf16[2,64,32,512]{3,2,1,0:T(8,128)(2,1)}, u32[]{:S(2)}) %copy-start) | copy-done | bytes 4194328
  4.3 0.9 %kl_stage.1 = (f32[4,2,16,512]{3,2,1,0:T(8,128)S(1)}, bf16[4,2,16,512]{3,2,1,0:T(8,128)(2,1)S(1)}) custom-call(bf16[2,64,1024]{2,1,0:T(8,128)(2,1)S(1)} %spread_stage.1.spread_ref, bf16[2,64,32,512]{3,2,1,0:T(8,128)(2,1)S(1)} %copy-done), custom_call_target="tpu_custom_call" | custom-call | flops 2000000000 | bytes 4096 | tf_op jit(solution)/shard_map/kl_stage/pallas_call | solution.py:124
  5.1 0.6 %collective-permute-start = (bf16[4,2,16,512]{3,2,1,0:T(8,128)(2,1)S(1)}, bf16[4,2,16,512]{3,2,1,0:T(8,128)(2,1)S(1)}, u32[]{:S(2)}, u32[]{:S(2)}) collective-permute-start(bf16[4,2,16,512]{3,2,1,0:T(8,128)(2,1)S(1)} %get-tuple-element.18), channel_id=1, source_target_pairs={{0,1},{1,0},{2,3},{3,2},{4,5},{5,4},{6,7},{7,6},{8,9},{9,8},{10,11... | collective-permute-start | bytes 393224 | tf_op jit(solution)/shard_map/ppermute | solution.py:480
  5.7 0.0 copy-done.3
  5.7 0.0 copy-done.4
  5.7 0.1 add_bitcast_fusion.in_ref
  5.8 2.5 %collective-permute-start.3 = (s32[1,10]{1,0:T(1,128)S(1)}, s32[1,10]{1,0:T(1,128)S(1)}, u32[]{:S(2)}, u32[]{:S(2)}) collective-permute-start(s32[1,10]{1,0:T(1,128)S(1)} %lead.1.low_ref), channel_id=1, source_target_pairs={{0,8},{8,0},{16,24},{24,16},{1,9},{9,1},{17,25},{25,17},{2,10},{10... | collective-permute-start | bytes 128 | tf_op jit(solution)/shard_map/ppermute | solution.py:480
  8.3 1.5 %collective-permute-done.3.high_ref = s32[1,10]{1,0:T(1,128)S(1)} collective-permute-done((s32[1,10]{1,0:T(1,128)S(1)}, s32[1,10]{1,0:T(1,128)S(1)}, u32[]{:S(2)}, u32[]{:S(2)}) %collective-permute-start.3) | collective-permute-done | bytes 72 | tf_op jit(solution)/shard_map/ppermute | solution.py:480
  9.9 2.0 %collective-permute-start.4 = (s32[2,10]{1,0:T(2,128)S(1)}, s32[2,10]{1,0:T(2,128)S(1)}, u32[]{:S(2)}, u32[]{:S(2)}) collective-permute-start(s32[2,10]{1,0:T(2,128)S(1)} %stack.2.low_ref), channel_id=1, source_target_pairs={{0,16},{8,24},{16,0},{24,8},{1,17},{9,25},{17,1},{25,9},{2,18},{10... | collective-permute-start | bytes 248 | tf_op jit(solution)/shard_map/ppermute | solution.py:480
  11.9 1.6 %collective-permute-done.4.high_ref = s32[2,10]{1,0:T(2,128)S(1)} collective-permute-done((s32[2,10]{1,0:T(2,128)S(1)}, s32[2,10]{1,0:T(2,128)S(1)}, u32[]{:S(2)}, u32[]{:S(2)}) %collective-permute-start.4) | collective-permute-done | bytes 112 | tf_op jit(solution)/shard_map/ppermute | solution.py:480
  13.5 0.0 collective-permute-done.got_ref
  13.5 2.1 %collective-permute-start.1 = (bf16[2,2,16,512]{3,2,1,0:T(8,128)(2,1)S(1)}, bf16[2,2,16,512]{3,2,1,0:T(8,128)(2,1)S(1)}, u32[]{:S(2)}, u32[]{:S(2)}) collective-permute-start(bf16[2,2,16,512]{3,2,1,0:T(8,128)(2,1)S(1)} %get-tuple-element.20), channel_id=1, source_target_pairs={{0,2},{1,3},{2,0},{3,1},{4,6},{5,7},{6,4},{7,5},{8,10},{9,11},{10,... | collective-permute-start | bytes 196616 | tf_op jit(solution)/shard_map/ppermute | solution.py:480
  15.7 2.1 %legendre_stage.1 = (bf16[128,1024]{1,0:T(8,128)(2,1)S(1)}, bf16[128,2048]{1,0:T(8,128)(2,1)S(1)}) custom-call(s32[4,10]{1,0:T(4,128)S(1)} %stack.3.ids_ref), custom_call_target="tpu_custom_call" | custom-call | flops 2000000000 | bytes 4096 | tf_op jit(solution)/shard_map/legendre_stage/pallas_call | solution.py:334
  17.7 0.2 collective-permute-done.1.got_ref
  17.9 3.5 %collective-permute-start.2 = (bf16[1,2,16,512]{3,2,1,0:T(8,128)(2,1)S(1)}, bf16[1,2,16,512]{3,2,1,0:T(8,128)(2,1)S(1)}, u32[]{:S(2)}, u32[]{:S(2)}) collective-permute-start(bf16[1,2,16,512]{3,2,1,0:T(8,128)(2,1)S(1)} %get-tuple-element.22), channel_id=1, source_target_pairs={{0,4},{1,5},{2,6},{3,7},{4,0},{5,1},{6,2},{7,3},{8,12},{9,13},{10,... | collective-permute-start | bytes 98312 | tf_op jit(solution)/shard_map/ppermute | solution.py:480
  21.4 0.0 slice-done
  21.4 0.0 slice-done.1
  21.4 2.1 %projection.1.folded_ref = bf16[2,128,512]{2,1,0:T(8,128)(2,1)S(1)} custom-call(s32[4,10]{1,0:T(4,128)S(1)} %stack.3.ids_ref, bf16[128,1024]{1,0:T(8,128)(2,1)S(1)} %get-tuple-element.23.turned_ref, bf16[2,4,1024,512]{3,2,1,0:T(8,128)(2,1)S(1)} %bitcast.3), custom_call_target="tpu_custom_call" | custom-call | flops 2000000000 | bytes 4096 | tf_op jit(solution)/shard_map/projection/pallas_call | solution.py:384
  23.5 0.0 collective-permute-done.2.got_ref
  23.5 0.2 cycle_values.1
  23.8 1.6 %collective-permute-start.5 = (bf16[32,128]{1,0:T(8,128)(2,1)S(1)}, bf16[32,128]{1,0:T(8,128)(2,1)S(1)}, u32[]{:S(2)}, u32[]{:S(2)}) collective-permute-start(bf16[32,128]{1,0:T(8,128)(2,1)S(1)} %get-tuple-element.25), channel_id=1, source_target_pairs={{0,8},{8,0},{16,24},{24,16},{1,9},{9,1},{17,25},{25,17},{2,10},{10... | collective-permute-start | bytes 24584 | tf_op jit(solution)/shard_map/ppermute | solution.py:480
  25.3 1.5 %collective-permute-start.6 = (bf16[32,128]{1,0:T(8,128)(2,1)S(1)}, bf16[32,128]{1,0:T(8,128)(2,1)S(1)}, u32[]{:S(2)}, u32[]{:S(2)}) collective-permute-start(bf16[32,128]{1,0:T(8,128)(2,1)S(1)} %get-tuple-element.26), channel_id=1, source_target_pairs={{0,16},{8,24},{16,0},{24,8},{1,17},{9,25},{17,1},{25,9},{2,18},{10... | collective-permute-start | bytes 24584 | tf_op jit(solution)/shard_map/ppermute | solution.py:480
  26.8 0.5 %collective-permute-start.7 = (bf16[32,128]{1,0:T(8,128)(2,1)S(1)}, bf16[32,128]{1,0:T(8,128)(2,1)S(1)}, u32[]{:S(2)}, u32[]{:S(2)}) collective-permute-start(bf16[32,128]{1,0:T(8,128)(2,1)S(1)} %get-tuple-element.27), channel_id=1, source_target_pairs={{0,24},{8,16},{16,8},{24,0},{1,25},{9,17},{17,9},{25,1},{2,26},{10... | collective-permute-start | bytes 24584 | tf_op jit(solution)/shard_map/ppermute | solution.py:480
  27.3 0.2 collective-permute-done.5.refs_1_
  27.5 1.5 %collective-permute-done.6.refs_2_ = bf16[32,128]{1,0:T(8,128)(2,1)S(1)} collective-permute-done((bf16[32,128]{1,0:T(8,128)(2,1)S(1)}, bf16[32,128]{1,0:T(8,128)(2,1)S(1)}, u32[]{:S(2)}, u32[]{:S(2)}) %collective-permute-start.6) | collective-permute-done | bytes 8224 | tf_op jit(solution)/shard_map/ppermute | solution.py:480
  29.0 2.4 %collective-permute-done.7.refs_3_ = bf16[32,128]{1,0:T(8,128)(2,1)S(1)} collective-permute-done((bf16[32,128]{1,0:T(8,128)(2,1)S(1)}, bf16[32,128]{1,0:T(8,128)(2,1)S(1)}, u32[]{:S(2)}, u32[]{:S(2)}) %collective-permute-start.7) | collective-permute-done | bytes 8224 | tf_op jit(solution)/shard_map/ppermute | solution.py:480
  31.4 1.0 %sky_maps.1 = f32[8,2,4,2048]{3,2,1,0:T(4,128)} custom-call(bf16[32,128]{1,0:T(8,128)(2,1)S(1)} %get-tuple-element.24.refs_0_, bf16[32,128]{1,0:T(8,128)(2,1)S(1)} %collective-permute-done.5.refs_1_, bf16[32,128]{1,0:T(8,128)(2,1)S(1)} %collective-permute-done.6.refs_2_, bf16[32,128]{1,0:T(8,128)(2,1)S(1)} %collective-permute-done.7.refs_3_, ...), custom_call_target="tpu_custom_call" | custom-call | tf_op jit(solution)/shard_map/sky_maps/pallas_call | solution.py:468
  (11 shorter events, 0.1 us)
Async XLA Ops:
  0.0 0.7 %copy-start.1 = (bf16[2,4,64]{2,1,0:T(4,128)(2,1)S(1)}, bf16[2,4,64]{2,1,0:T(4,128)(2,1)}, u32[]{:S(2)}) copy-start(bf16[2,4,64]{2,1,0:T(4,128)(2,1)} %coeff_ref.1) | copy-start | bytes 3076
  0.7 0.7 %copy-start.2 = (s32[2]{0:T(128)S(1)}, s32[2]{0:T(128)}, u32[]{:S(2)}) copy-start(s32[2]{0:T(128)} %kept_ref.1) | copy-start | bytes 28
  1.3 4.4 %copy-start.3 = (s32[8]{0:T(128)S(1)}, s32[8]{0:T(128)}, u32[]{:S(2)}) copy-start(s32[8]{0:T(128)} %param.8) | copy-start | bytes 100
  1.3 4.4 %copy-start.4 = (s32[2]{0:T(128)S(1)}, s32[2]{0:T(128)}, u32[]{:S(2)}) copy-start(s32[2]{0:T(128)} %param.6) | copy-start | bytes 28
  2.1 2.2 %copy-start = (bf16[2,64,32,512]{3,2,1,0:T(8,128)(2,1)S(1)}, bf16[2,64,32,512]{3,2,1,0:T(8,128)(2,1)}, u32[]{:S(2)}) copy-start(bf16[2,64,32,512]{3,2,1,0:T(8,128)(2,1)} %vectors_ref.1) | copy-start | bytes 12582916
  5.1 8.3 %collective-permute-start = (bf16[4,2,16,512]{3,2,1,0:T(8,128)(2,1)S(1)}, bf16[4,2,16,512]{3,2,1,0:T(8,128)(2,1)S(1)}, u32[]{:S(2)}, u32[]{:S(2)}) collective-permute-start(bf16[4,2,16,512]{3,2,1,0:T(8,128)(2,1)S(1)} %get-tuple-element.18), channel_id=1, source_target_pairs={{0,1},{1,0},{2,3},{3,2},{4,5},{5,4},{6,7},{7,6},{8,9},{9,8},{10,11... | collective-permute-start | bytes 393224 | tf_op jit(solution)/shard_map/ppermute | solution.py:480
  5.7 15.7 %slice-start = ((s8[8388608]{0:T(1024)(128)(4,1)}), s8[4194304]{0:T(1024)(128)(4,1)S(1)}, s32[]{:S(2)}) async-start(s8[8388608]{0:T(1024)(128)(4,1)} %bitcast.2), calls=%async_computation | async-start | bytes 8388608
  5.8 15.6 %slice-start.1 = ((s8[8388608]{0:T(1024)(128)(4,1)}), s8[4194304]{0:T(1024)(128)(4,1)S(1)}, s32[]{:S(2)}) async-start(s8[8388608]{0:T(1024)(128)(4,1)} %bitcast.2), calls=%async_computation.1 | async-start | bytes 8388608
  5.8 4.1 %collective-permute-start.3 = (s32[1,10]{1,0:T(1,128)S(1)}, s32[1,10]{1,0:T(1,128)S(1)}, u32[]{:S(2)}, u32[]{:S(2)}) collective-permute-start(s32[1,10]{1,0:T(1,128)S(1)} %lead.1.low_ref), channel_id=1, source_target_pairs={{0,8},{8,0},{16,24},{24,16},{1,9},{9,1},{17,25},{25,17},{2,10},{10... | collective-permute-start | bytes 128 | tf_op jit(solution)/shard_map/ppermute | solution.py:480
  9.9 3.6 %collective-permute-start.4 = (s32[2,10]{1,0:T(2,128)S(1)}, s32[2,10]{1,0:T(2,128)S(1)}, u32[]{:S(2)}, u32[]{:S(2)}) collective-permute-start(s32[2,10]{1,0:T(2,128)S(1)} %stack.2.low_ref), channel_id=1, source_target_pairs={{0,16},{8,24},{16,0},{24,8},{1,17},{9,25},{17,1},{25,9},{2,18},{10... | collective-permute-start | bytes 248 | tf_op jit(solution)/shard_map/ppermute | solution.py:480
  13.5 4.4 %collective-permute-start.1 = (bf16[2,2,16,512]{3,2,1,0:T(8,128)(2,1)S(1)}, bf16[2,2,16,512]{3,2,1,0:T(8,128)(2,1)S(1)}, u32[]{:S(2)}, u32[]{:S(2)}) collective-permute-start(bf16[2,2,16,512]{3,2,1,0:T(8,128)(2,1)S(1)} %get-tuple-element.20), channel_id=1, source_target_pairs={{0,2},{1,3},{2,0},{3,1},{4,6},{5,7},{6,4},{7,5},{8,10},{9,11},{10,... | collective-permute-start | bytes 196616 | tf_op jit(solution)/shard_map/ppermute | solution.py:480
  17.9 5.6 %collective-permute-start.2 = (bf16[1,2,16,512]{3,2,1,0:T(8,128)(2,1)S(1)}, bf16[1,2,16,512]{3,2,1,0:T(8,128)(2,1)S(1)}, u32[]{:S(2)}, u32[]{:S(2)}) collective-permute-start(bf16[1,2,16,512]{3,2,1,0:T(8,128)(2,1)S(1)} %get-tuple-element.22), channel_id=1, source_target_pairs={{0,4},{1,5},{2,6},{3,7},{4,0},{5,1},{6,2},{7,3},{8,12},{9,13},{10,... | collective-permute-start | bytes 98312 | tf_op jit(solution)/shard_map/ppermute | solution.py:480
  23.8 3.7 %collective-permute-start.5 = (bf16[32,128]{1,0:T(8,128)(2,1)S(1)}, bf16[32,128]{1,0:T(8,128)(2,1)S(1)}, u32[]{:S(2)}, u32[]{:S(2)}) collective-permute-start(bf16[32,128]{1,0:T(8,128)(2,1)S(1)} %get-tuple-element.25), channel_id=1, source_target_pairs={{0,8},{8,0},{16,24},{24,16},{1,9},{9,1},{17,25},{25,17},{2,10},{10... | collective-permute-start | bytes 24584 | tf_op jit(solution)/shard_map/ppermute | solution.py:480
  25.3 3.7 %collective-permute-start.6 = (bf16[32,128]{1,0:T(8,128)(2,1)S(1)}, bf16[32,128]{1,0:T(8,128)(2,1)S(1)}, u32[]{:S(2)}, u32[]{:S(2)}) collective-permute-start(bf16[32,128]{1,0:T(8,128)(2,1)S(1)} %get-tuple-element.26), channel_id=1, source_target_pairs={{0,16},{8,24},{16,0},{24,8},{1,17},{9,25},{17,1},{25,9},{2,18},{10... | collective-permute-start | bytes 24584 | tf_op jit(solution)/shard_map/ppermute | solution.py:480
  26.8 4.5 %collective-permute-start.7 = (bf16[32,128]{1,0:T(8,128)(2,1)S(1)}, bf16[32,128]{1,0:T(8,128)(2,1)S(1)}, u32[]{:S(2)}, u32[]{:S(2)}) collective-permute-start(bf16[32,128]{1,0:T(8,128)(2,1)S(1)} %get-tuple-element.27), channel_id=1, source_target_pairs={{0,24},{8,16},{16,8},{24,0},{1,25},{9,17},{17,9},{25,1},{2,26},{10... | collective-permute-start | bytes 24584 | tf_op jit(solution)/shard_map/ppermute | solution.py:480

commit v4 on v3

--- a/solution.py
+++ b/solution.py
@@ -14,7 +14,7 @@
 NSIDE = 512
 PARTS = 4
 BLOCKS = 32
-STEPS = L // BLOCKS
+STEPS = L // BLOCKS + 1
 ROWS = 256
 LANES = 128
 CHUNKS = 4
@@ -296,7 +296,7 @@
 
 
 def legendre_kernel(
-    slots, per_slot, ids_ref, turned_ref, fourier_ref, p_ref, q_ref, left, right, scale, table
+    slots, ids_ref, turned_ref, p_ref, q_ref, left, right, scale, table
 ):
     members, entries = ids_ref.shape
     cycles_each = entries - slots
@@ -313,8 +313,11 @@
     cosine, sine = angles(cycle.astype(f32))
     legendre_rows(m.astype(f32), cosine, sine, p_ref, q_ref, left, right, scale, table)
     for j in range(width // LANES):
-        turned_ref[j * LANES : (j + 1) * LANES] = table[j].T.astype(bf16)
-
+        turned_ref[j * LANES : (j + 1) * LANES] = table[j, :L].T.astype(bf16)
+
+
+def fourier_kernel(slots, per_slot, ids_ref, fourier_ref):
+    members = ids_ref.shape[0]
     every = members * slots
     row = iota((every, 1), 0)
     m_every = jnp.zeros((every, 1), jnp.int32)
@@ -328,24 +331,34 @@
         fourier_ref[j * per_slot : (j + 1) * per_slot] = rows.astype(bf16)
 
 
-def legendre_stage(ids, slots, per_slot):
+def fourier_stage(ids, slots, per_slot):
+    rows = ids.shape[0] * slots * per_slot
+    return pl.pallas_call(
+        functools.partial(fourier_kernel, slots, per_slot),
+        out_shape=jax.ShapeDtypeStruct((rows, NPHI), bf16),
+        in_specs=[SMEM],
+        out_specs=VMEM,
+        compiler_params=pltpu.CompilerParams(vmem_limit_bytes=LIMIT),
+        cost_estimate=work(0.5),
+        name="fourier_stage",
+    )(ids)
+
+
+def legendre_stage(ids, slots):
     members, entries = ids.shape
     width = padded(slots * members * (entries - slots))
     return pl.pallas_call(
-        functools.partial(legendre_kernel, slots, per_slot),
-        out_shape=(
-            jax.ShapeDtypeStruct((width, L), bf16),
-            jax.ShapeDtypeStruct((members * slots * per_slot, NPHI), bf16),
-        ),
+        functools.partial(legendre_kernel, slots),
+        out_shape=jax.ShapeDtypeStruct((width, L), bf16),
         in_specs=[SMEM],
-        out_specs=(VMEM, VMEM),
+        out_specs=VMEM,
         scratch_shapes=[
             pltpu.VMEM((STEPS, BLOCKS, width), f32),
             pltpu.VMEM((STEPS, BLOCKS, width), f32),
             pltpu.VMEM((BLOCKS, width), f32),
             pltpu.VMEM((BLOCKS, width), f32),
             pltpu.VMEM((BLOCKS, width), f32),
-            pltpu.VMEM((width // LANES, L, LANES), f32),
+            pltpu.VMEM((width // LANES, BLOCKS * STEPS, LANES), f32),
         ],
         compiler_params=pltpu.CompilerParams(vmem_limit_bytes=LIMIT),
         cost_estimate=work(2.0),
@@ -354,29 +367,36 @@
 
 
 def projection_kernel(ids_ref, turned_ref, beam_ref, folded_ref, sums, woven):
-    slots, share, cycles, depth = sums.shape
-    sums[...] = jnp.zeros_like(sums)
-    for t in reversed(range(L // ROWS)):
-        for s in range(slots):
-
-            @pl.when(ids_ref[0, s] < (t + 1) * ROWS)
-            def _():
-                lhs = turned_ref[s * cycles : (s + 1) * cycles, t * ROWS : (t + 1) * ROWS]
-                for c in range(share):
-                    sums[s, c] += jnp.dot(
-                        lhs,
-                        beam_ref[s, c, t * ROWS : (t + 1) * ROWS, :],
-                        preferred_element_type=f32,
-                    )
-
-    for s in range(slots):
-        for c in range(share):
+    slots, share, _, depth = beam_ref.shape
+    cycles = folded_ref.shape[1] // share
+    last = L // ROWS
+    for pair in range(0, slots, 2):
+        low = ids_ref[0, pair] // ROWS
+        counts = last - low
+        for k in range(last + 1):
+            first = (k < counts).astype(jnp.int32)
+            slot = pair + 1 - first
+            start = jnp.where(k < counts, low + k, last - 1 - low + k - counts)
+            start = pl.multiple_of(start * ROWS, ROWS)
+            lhs = turned_ref[
+                pl.ds(pl.multiple_of(slot * cycles, cycles), cycles), pl.ds(start, ROWS)
+            ]
+            for c in range(share):
+                sums[k, c] = jnp.dot(
+                    lhs, beam_ref[slot, c, pl.ds(start, ROWS), :], preferred_element_type=f32
+                )
+        for s in range(2):
+            for c in range(share):
+                total = jnp.zeros((cycles, depth), f32)
+                for k in range(last + 1):
+                    mine = (k < counts) if s == 0 else (k >= counts)
+                    total = total + jnp.where(mine, sums[k, c], 0.0)
+                for j in range(depth // LANES):
+                    woven[s, j, pl.ds(c, cycles, stride=share), :] = total[
+                        :, j * LANES : (j + 1) * LANES
+                    ]
             for j in range(depth // LANES):
-                woven[s, j, pl.ds(c, cycles, stride=share), :] = sums[
-                    s, c, :, j * LANES : (j + 1) * LANES
-                ]
-        for j in range(depth // LANES):
-            folded_ref[s, :, j * LANES : (j + 1) * LANES] = woven[s, j].astype(bf16)
+                folded_ref[pair + s, :, j * LANES : (j + 1) * LANES] = woven[s, j].astype(bf16)
 
 
 def projection(ids, turned, beam, cycles):
@@ -387,8 +407,8 @@
         in_specs=[SMEM, VMEM, VMEM],
         out_specs=VMEM,
         scratch_shapes=[
-            pltpu.VMEM((slots, share, cycles, depth), f32),
-            pltpu.VMEM((slots, depth // LANES, cycles * share, LANES), f32),
+            pltpu.VMEM((L // ROWS + 1, share, cycles, depth), f32),
+            pltpu.VMEM((2, depth // LANES, cycles * share, LANES), f32),
         ],
         compiler_params=pltpu.CompilerParams(vmem_limit_bytes=LIMIT),
         cost_estimate=work(2.0),
@@ -497,7 +517,8 @@
         if bit == pieces:
             break
         held, send = fold_stage(bit, held, got)
-    turned, fourier = legendre_stage(ids, slots, share * PARTS)
+    turned = legendre_stage(ids, slots)
+    fourier = fourier_stage(ids, slots, share * PARTS)
     folded = projection(ids, turned, beam_matrix, members * cycle_ids.shape[0])
     values = cycle_values(held, got, folded, members)
     gathered = [values[0]]

time: 32.5 us -> 32.3 us (level)
    pallas_call x1, Pallas kernels: 2.11 us -> 1.67 us  [projection(): pl.pallas_call(projection_kernel, out_shape=jax.ShapeDtypeStruct((slots,...]
    pallas_call x1 -> x2, Pallas kernels: 2.06 us -> 2.34 us  [the longest x1 1.56 us: legendre_stage(): pl.pallas_call(functools.partial(legendre_kernel, slots), out_shape=jax.S...]
where the time goes in v4:
time: 32.3 us; the launch traced here: 32.1 us
  starting transfers between devices  14.3 us (44%)
  waiting for transfers between devices  7.28 us (23%)
  Pallas kernels  6.87 us (21%)
  local copies, waits for them, and re-layouts  3.53 us (11%)
    ppermute x8, starting transfers between devices, swap(): return lax.ppermute(value, axis, [(k, k ^ bit) for k in range(size)])  14.3 us
    ppermute x8, waiting for transfers between devices, swap(): return lax.ppermute(value, axis, [(k, k ^ bit) for k in range(size)])  7.28 us
    unnamed x14, local copies, waits for them, and re-layouts  3.53 us
    pallas_call x1, Pallas kernels, projection(): pl.pallas_call(projection_kernel, out_shape=jax.ShapeDtypeStruct((slots,...  1.67 us
    pallas_call x1, Pallas kernels, legendre_stage(): pl.pallas_call(functools.partial(legendre_kernel, slots), out_shape=jax.S...  1.56 us
    pallas_call x1, Pallas kernels, sky_maps(): pl.pallas_call(functools.partial(sky_kernel, members), out_shape=jax.Shap...  0.98 us
    pallas_call x1, Pallas kernels, kl_stage(): pl.pallas_call(kl_kernel, out_shape=(jax.ShapeDtypeStruct(shape, f32), ja...  0.85 us
    pallas_call x1, Pallas kernels, fourier_stage(): pl.pallas_call(functools.partial(fourier_kernel, slots, per_slot), out_sh...  0.78 us
  transfers between devices with their start and end apart: 8, of which 6 were waited for; matrix products, arithmetic and copies ran while one was open for 0% of the time, Pallas kernels for 13%

profile of v4, /device:TPU:0, one launch (start us, length us, event | category | flops | bytes accessed | tf_op | source)
XLA Modules:
  0.0 32.1 jit_solution(14689230587208655017)
XLA Ops:
  0.0 0.7 %copy-done.1 = bf16[2,4,64]{2,1,0:T(4,128)(2,1)S(1)} copy-done((bf16[2,4,64]{2,1,0:T(4,128)(2,1)S(1)}, bf16[2,4,64]{2,1,0:T(4,128)(2,1)}, u32[]{:S(2)}) %copy-start.1) | copy-done | bytes 1048
  0.7 0.7 %copy-done.2 = s32[2]{0:T(128)S(1)} copy-done((s32[2]{0:T(128)S(1)}, s32[2]{0:T(128)}, u32[]{:S(2)}) %copy-start.2) | copy-done | bytes 32
  1.3 0.7 %spread_stage.1.spread_ref = bf16[2,64,1024]{2,1,0:T(8,128)(2,1)S(1)} custom-call(s32[2]{0:T(128)S(1)} %copy-done.2, bf16[2,4,64]{2,1,0:T(4,128)(2,1)S(1)} %copy-done.1), custom_call_target="tpu_custom_call" | custom-call | flops 1000000000 | bytes 4096 | tf_op jit(solution)/shard_map/spread_stage/pallas_call | solution.py:89
  2.1 0.0 copy-start
  2.1 2.2 %copy-done = bf16[2,64,32,512]{3,2,1,0:T(8,128)(2,1)S(1)} copy-done((bf16[2,64,32,512]{3,2,1,0:T(8,128)(2,1)S(1)}, bf16[2,64,32,512]{3,2,1,0:T(8,128)(2,1)}, u32[]{:S(2)}) %copy-start) | copy-done | bytes 4194328
  4.3 0.9 %kl_stage.1 = (f32[4,2,16,512]{3,2,1,0:T(8,128)S(1)}, bf16[4,2,16,512]{3,2,1,0:T(8,128)(2,1)S(1)}) custom-call(bf16[2,64,1024]{2,1,0:T(8,128)(2,1)S(1)} %spread_stage.1.spread_ref, bf16[2,64,32,512]{3,2,1,0:T(8,128)(2,1)S(1)} %copy-done), custom_call_target="tpu_custom_call" | custom-call | flops 2000000000 | bytes 4096 | tf_op jit(solution)/shard_map/kl_stage/pallas_call | solution.py:124
  5.1 0.6 %collective-permute-start = (bf16[4,2,16,512]{3,2,1,0:T(8,128)(2,1)S(1)}, bf16[4,2,16,512]{3,2,1,0:T(8,128)(2,1)S(1)}, u32[]{:S(2)}, u32[]{:S(2)}) collective-permute-start(bf16[4,2,16,512]{3,2,1,0:T(8,128)(2,1)S(1)} %get-tuple-element.16), channel_id=1, source_target_pairs={{0,1},{1,0},{2,3},{3,2},{4,5},{5,4},{6,7},{7,6},{8,9},{9,8},{10,11... | collective-permute-start | bytes 393224 | tf_op jit(solution)/shard_map/ppermute | solution.py:500
  5.7 0.0 copy-done.3
  5.7 0.0 copy-done.4
  5.7 0.1 add_bitcast_fusion.in_ref
  5.8 2.5 %collective-permute-start.3 = (s32[1,10]{1,0:T(1,128)S(1)}, s32[1,10]{1,0:T(1,128)S(1)}, u32[]{:S(2)}, u32[]{:S(2)}) collective-permute-start(s32[1,10]{1,0:T(1,128)S(1)} %lead.1.low_ref), channel_id=1, source_target_pairs={{0,8},{8,0},{16,24},{24,16},{1,9},{9,1},{17,25},{25,17},{2,10},{10... | collective-permute-start | bytes 128 | tf_op jit(solution)/shard_map/ppermute | solution.py:500
  8.3 1.5 %collective-permute-done.3.high_ref = s32[1,10]{1,0:T(1,128)S(1)} collective-permute-done((s32[1,10]{1,0:T(1,128)S(1)}, s32[1,10]{1,0:T(1,128)S(1)}, u32[]{:S(2)}, u32[]{:S(2)}) %collective-permute-start.3) | collective-permute-done | bytes 72 | tf_op jit(solution)/shard_map/ppermute | solution.py:500
  9.9 2.0 %collective-permute-start.4 = (s32[2,10]{1,0:T(2,128)S(1)}, s32[2,10]{1,0:T(2,128)S(1)}, u32[]{:S(2)}, u32[]{:S(2)}) collective-permute-start(s32[2,10]{1,0:T(2,128)S(1)} %stack.2.low_ref), channel_id=1, source_target_pairs={{0,16},{8,24},{16,0},{24,8},{1,17},{9,25},{17,1},{25,9},{2,18},{10... | collective-permute-start | bytes 248 | tf_op jit(solution)/shard_map/ppermute | solution.py:500
  11.9 1.6 %collective-permute-done.4.high_ref = s32[2,10]{1,0:T(2,128)S(1)} collective-permute-done((s32[2,10]{1,0:T(2,128)S(1)}, s32[2,10]{1,0:T(2,128)S(1)}, u32[]{:S(2)}, u32[]{:S(2)}) %collective-permute-start.4) | collective-permute-done | bytes 112 | tf_op jit(solution)/shard_map/ppermute | solution.py:500
  13.5 0.0 collective-permute-done.got_ref
  13.5 2.1 %collective-permute-start.1 = (bf16[2,2,16,512]{3,2,1,0:T(8,128)(2,1)S(1)}, bf16[2,2,16,512]{3,2,1,0:T(8,128)(2,1)S(1)}, u32[]{:S(2)}, u32[]{:S(2)}) collective-permute-start(bf16[2,2,16,512]{3,2,1,0:T(8,128)(2,1)S(1)} %get-tuple-element.18), channel_id=1, source_target_pairs={{0,2},{1,3},{2,0},{3,1},{4,6},{5,7},{6,4},{7,5},{8,10},{9,11},{10,... | collective-permute-start | bytes 196616 | tf_op jit(solution)/shard_map/ppermute | solution.py:500
  15.7 1.6 %legendre_stage.1.turned_ref = bf16[128,1024]{1,0:T(8,128)(2,1)S(1)} custom-call(s32[4,10]{1,0:T(4,128)S(1)} %stack.3.ids_ref), custom_call_target="tpu_custom_call" | custom-call | flops 2000000000 | bytes 4096 | tf_op jit(solution)/shard_map/legendre_stage/pallas_call | solution.py:350
  17.2 0.7 %collective-permute-done.1.got_ref = bf16[2,2,16,512]{3,2,1,0:T(8,128)(2,1)S(1)} collective-permute-done((bf16[2,2,16,512]{3,2,1,0:T(8,128)(2,1)S(1)}, bf16[2,2,16,512]{3,2,1,0:T(8,128)(2,1)S(1)}, u32[]{:S(2)}, u32[]{:S(2)}) %collective-permute-start.1) | collective-permute-done | bytes 65568 | tf_op jit(solution)/shard_map/ppermute | solution.py:500
  17.9 3.5 %collective-permute-start.2 = (bf16[1,2,16,512]{3,2,1,0:T(8,128)(2,1)S(1)}, bf16[1,2,16,512]{3,2,1,0:T(8,128)(2,1)S(1)}, u32[]{:S(2)}, u32[]{:S(2)}) collective-permute-start(bf16[1,2,16,512]{3,2,1,0:T(8,128)(2,1)S(1)} %get-tuple-element.20), channel_id=1, source_target_pairs={{0,4},{1,5},{2,6},{3,7},{4,0},{5,1},{6,2},{7,3},{8,12},{9,13},{10,... | collective-permute-start | bytes 98312 | tf_op jit(solution)/shard_map/ppermute | solution.py:500
  21.4 0.0 slice-done
  21.4 0.0 slice-done.1
  21.4 1.7 %projection.1.folded_ref = bf16[2,128,512]{2,1,0:T(8,128)(2,1)S(1)} custom-call(s32[4,10]{1,0:T(4,128)S(1)} %stack.3.ids_ref, bf16[128,1024]{1,0:T(8,128)(2,1)S(1)} %legendre_stage.1.turned_ref, bf16[2,4,1024,512]{3,2,1,0:T(8,128)(2,1)S(1)} %bitcast.3), custom_call_target="tpu_custom_call" | custom-call | flops 2000000000 | bytes 4096 | tf_op jit(solution)/shard_map/projection/pallas_call | solution.py:404
  23.1 0.2 collective-permute-done.2.got_ref
  23.3 0.2 cycle_values.1
  23.5 1.6 %collective-permute-start.5 = (bf16[32,128]{1,0:T(8,128)(2,1)S(1)}, bf16[32,128]{1,0:T(8,128)(2,1)S(1)}, u32[]{:S(2)}, u32[]{:S(2)}) collective-permute-start(bf16[32,128]{1,0:T(8,128)(2,1)S(1)} %get-tuple-element.22), channel_id=1, source_target_pairs={{0,8},{8,0},{16,24},{24,16},{1,9},{9,1},{17,25},{25,17},{2,10},{10... | collective-permute-start | bytes 24584 | tf_op jit(solution)/shard_map/ppermute | solution.py:500
  25.1 1.5 %collective-permute-start.6 = (bf16[32,128]{1,0:T(8,128)(2,1)S(1)}, bf16[32,128]{1,0:T(8,128)(2,1)S(1)}, u32[]{:S(2)}, u32[]{:S(2)}) collective-permute-start(bf16[32,128]{1,0:T(8,128)(2,1)S(1)} %get-tuple-element.23), channel_id=1, source_target_pairs={{0,16},{8,24},{16,0},{24,8},{1,17},{9,25},{17,1},{25,9},{2,18},{10... | collective-permute-start | bytes 24584 | tf_op jit(solution)/shard_map/ppermute | solution.py:500
  26.6 0.5 %collective-permute-start.7 = (bf16[32,128]{1,0:T(8,128)(2,1)S(1)}, bf16[32,128]{1,0:T(8,128)(2,1)S(1)}, u32[]{:S(2)}, u32[]{:S(2)}) collective-permute-start(bf16[32,128]{1,0:T(8,128)(2,1)S(1)} %get-tuple-element.24), channel_id=1, source_target_pairs={{0,24},{8,16},{16,8},{24,0},{1,25},{9,17},{17,9},{25,1},{2,26},{10... | collective-permute-start | bytes 24584 | tf_op jit(solution)/shard_map/ppermute | solution.py:500
  27.1 0.8 %fourier_stage.1.refs_4_ = bf16[128,2048]{1,0:T(8,128)(2,1)S(1)} custom-call(s32[4,10]{1,0:T(4,128)S(1)} %stack.3.ids_ref), custom_call_target="tpu_custom_call" | custom-call | flops 500000000 | bytes 4096 | tf_op jit(solution)/shard_map/fourier_stage/pallas_call | solution.py:336
  27.9 0.0 collective-permute-done.5.refs_1_
  27.9 0.9 %collective-permute-done.6.refs_2_ = bf16[32,128]{1,0:T(8,128)(2,1)S(1)} collective-permute-done((bf16[32,128]{1,0:T(8,128)(2,1)S(1)}, bf16[32,128]{1,0:T(8,128)(2,1)S(1)}, u32[]{:S(2)}, u32[]{:S(2)}) %collective-permute-start.6) | collective-permute-done | bytes 8224 | tf_op jit(solution)/shard_map/ppermute | solution.py:500
  28.7 2.4 %collective-permute-done.7.refs_3_ = bf16[32,128]{1,0:T(8,128)(2,1)S(1)} collective-permute-done((bf16[32,128]{1,0:T(8,128)(2,1)S(1)}, bf16[32,128]{1,0:T(8,128)(2,1)S(1)}, u32[]{:S(2)}, u32[]{:S(2)}) %collective-permute-start.7) | collective-permute-done | bytes 8224 | tf_op jit(solution)/shard_map/ppermute | solution.py:500
  31.1 1.0 %sky_maps.1 = f32[8,2,4,2048]{3,2,1,0:T(4,128)} custom-call(bf16[32,128]{1,0:T(8,128)(2,1)S(1)} %get-tuple-element.21.refs_0_, bf16[32,128]{1,0:T(8,128)(2,1)S(1)} %collective-permute-done.5.refs_1_, bf16[32,128]{1,0:T(8,128)(2,1)S(1)} %collective-permute-done.6.refs_2_, bf16[32,128]{1,0:T(8,128)(2,1)S(1)} %collective-permute-done.7.refs_3_, ...), custom_call_target="tpu_custom_call" | custom-call | tf_op jit(solution)/shard_map/sky_maps/pallas_call | solution.py:488
  (12 shorter events, 0.1 us)
Async XLA Ops:
  0.0 0.7 %copy-start.1 = (bf16[2,4,64]{2,1,0:T(4,128)(2,1)S(1)}, bf16[2,4,64]{2,1,0:T(4,128)(2,1)}, u32[]{:S(2)}) copy-start(bf16[2,4,64]{2,1,0:T(4,128)(2,1)} %coeff_ref.1) | copy-start | bytes 3076
  0.7 0.7 %copy-start.2 = (s32[2]{0:T(128)S(1)}, s32[2]{0:T(128)}, u32[]{:S(2)}) copy-start(s32[2]{0:T(128)} %kept_ref.1) | copy-start | bytes 28
  1.3 4.4 %copy-start.3 = (s32[8]{0:T(128)S(1)}, s32[8]{0:T(128)}, u32[]{:S(2)}) copy-start(s32[8]{0:T(128)} %param.8) | copy-start | bytes 100
  1.3 4.4 %copy-start.4 = (s32[2]{0:T(128)S(1)}, s32[2]{0:T(128)}, u32[]{:S(2)}) copy-start(s32[2]{0:T(128)} %param.6) | copy-start | bytes 28
  2.1 2.2 %copy-start = (bf16[2,64,32,512]{3,2,1,0:T(8,128)(2,1)S(1)}, bf16[2,64,32,512]{3,2,1,0:T(8,128)(2,1)}, u32[]{:S(2)}) copy-start(bf16[2,64,32,512]{3,2,1,0:T(8,128)(2,1)} %vectors_ref.1) | copy-start | bytes 12582916
  5.1 8.3 %collective-permute-start = (bf16[4,2,16,512]{3,2,1,0:T(8,128)(2,1)S(1)}, bf16[4,2,16,512]{3,2,1,0:T(8,128)(2,1)S(1)}, u32[]{:S(2)}, u32[]{:S(2)}) collective-permute-start(bf16[4,2,16,512]{3,2,1,0:T(8,128)(2,1)S(1)} %get-tuple-element.16), channel_id=1, source_target_pairs={{0,1},{1,0},{2,3},{3,2},{4,5},{5,4},{6,7},{7,6},{8,9},{9,8},{10,11... | collective-permute-start | bytes 393224 | tf_op jit(solution)/shard_map/ppermute | solution.py:500
  5.7 15.7 %slice-start = ((s8[8388608]{0:T(1024)(128)(4,1)}), s8[4194304]{0:T(1024)(128)(4,1)S(1)}, s32[]{:S(2)}) async-start(s8[8388608]{0:T(1024)(128)(4,1)} %bitcast.2), calls=%async_computation | async-start | bytes 8388608
  5.8 15.6 %slice-start.1 = ((s8[8388608]{0:T(1024)(128)(4,1)}), s8[4194304]{0:T(1024)(128)(4,1)S(1)}, s32[]{:S(2)}) async-start(s8[8388608]{0:T(1024)(128)(4,1)} %bitcast.2), calls=%async_computation.1 | async-start | bytes 8388608
  5.8 4.1 %collective-permute-start.3 = (s32[1,10]{1,0:T(1,128)S(1)}, s32[1,10]{1,0:T(1,128)S(1)}, u32[]{:S(2)}, u32[]{:S(2)}) collective-permute-start(s32[1,10]{1,0:T(1,128)S(1)} %lead.1.low_ref), channel_id=1, source_target_pairs={{0,8},{8,0},{16,24},{24,16},{1,9},{9,1},{17,25},{25,17},{2,10},{10... | collective-permute-start | bytes 128 | tf_op jit(solution)/shard_map/ppermute | solution.py:500
  9.9 3.6 %collective-permute-start.4 = (s32[2,10]{1,0:T(2,128)S(1)}, s32[2,10]{1,0:T(2,128)S(1)}, u32[]{:S(2)}, u32[]{:S(2)}) collective-permute-start(s32[2,10]{1,0:T(2,128)S(1)} %stack.2.low_ref), channel_id=1, source_target_pairs={{0,16},{8,24},{16,0},{24,8},{1,17},{9,25},{17,1},{25,9},{2,18},{10... | collective-permute-start | bytes 248 | tf_op jit(solution)/shard_map/ppermute | solution.py:500
  13.5 4.4 %collective-permute-start.1 = (bf16[2,2,16,512]{3,2,1,0:T(8,128)(2,1)S(1)}, bf16[2,2,16,512]{3,2,1,0:T(8,128)(2,1)S(1)}, u32[]{:S(2)}, u32[]{:S(2)}) collective-permute-start(bf16[2,2,16,512]{3,2,1,0:T(8,128)(2,1)S(1)} %get-tuple-element.18), channel_id=1, source_target_pairs={{0,2},{1,3},{2,0},{3,1},{4,6},{5,7},{6,4},{7,5},{8,10},{9,11},{10,... | collective-permute-start | bytes 196616 | tf_op jit(solution)/shard_map/ppermute | solution.py:500
  17.9 5.3 %collective-permute-start.2 = (bf16[1,2,16,512]{3,2,1,0:T(8,128)(2,1)S(1)}, bf16[1,2,16,512]{3,2,1,0:T(8,128)(2,1)S(1)}, u32[]{:S(2)}, u32[]{:S(2)}) collective-permute-start(bf16[1,2,16,512]{3,2,1,0:T(8,128)(2,1)S(1)} %get-tuple-element.20), channel_id=1, source_target_pairs={{0,4},{1,5},{2,6},{3,7},{4,0},{5,1},{6,2},{7,3},{8,12},{9,13},{10,... | collective-permute-start | bytes 98312 | tf_op jit(solution)/shard_map/ppermute | solution.py:500
  23.5 4.3 %collective-permute-start.5 = (bf16[32,128]{1,0:T(8,128)(2,1)S(1)}, bf16[32,128]{1,0:T(8,128)(2,1)S(1)}, u32[]{:S(2)}, u32[]{:S(2)}) collective-permute-start(bf16[32,128]{1,0:T(8,128)(2,1)S(1)} %get-tuple-element.22), channel_id=1, source_target_pairs={{0,8},{8,0},{16,24},{24,16},{1,9},{9,1},{17,25},{25,17},{2,10},{10... | collective-permute-start | bytes 24584 | tf_op jit(solution)/shard_map/ppermute | solution.py:500
  25.1 3.7 %collective-permute-start.6 = (bf16[32,128]{1,0:T(8,128)(2,1)S(1)}, bf16[32,128]{1,0:T(8,128)(2,1)S(1)}, u32[]{:S(2)}, u32[]{:S(2)}) collective-permute-start(bf16[32,128]{1,0:T(8,128)(2,1)S(1)} %get-tuple-element.23), channel_id=1, source_target_pairs={{0,16},{8,24},{16,0},{24,8},{1,17},{9,25},{17,1},{25,9},{2,18},{10... | collective-permute-start | bytes 24584 | tf_op jit(solution)/shard_map/ppermute | solution.py:500
  26.6 4.5 %collective-permute-start.7 = (bf16[32,128]{1,0:T(8,128)(2,1)S(1)}, bf16[32,128]{1,0:T(8,128)(2,1)S(1)}, u32[]{:S(2)}, u32[]{:S(2)}) collective-permute-start(bf16[32,128]{1,0:T(8,128)(2,1)S(1)} %get-tuple-element.24), channel_id=1, source_target_pairs={{0,24},{8,16},{16,8},{24,0},{1,25},{9,17},{17,9},{25,1},{2,26},{10... | collective-permute-start | bytes 24584 | tf_op jit(solution)/shard_map/ppermute | solution.py:500

commit v5 on v4

--- a/solution.py
+++ b/solution.py
@@ -55,7 +55,7 @@
         in_specs=[VMEM],
         out_specs=VMEM,
         compiler_params=pltpu.CompilerParams(vmem_limit_bytes=SMALL),
-        cost_estimate=work(4.0),
+        cost_estimate=work(3.0),
         name="lead",
     )(ids)
 
@@ -69,8 +69,8 @@
     mode_index = place * modes + iota((PARTS, modes), 1)
     tall = []
     for s in range(slots):
-        masked = jnp.where(mode_index < kept_ref[s], coeff_ref[s].astype(f32), 0.0)
-        tall += [masked] * group
+        kept = mode_index < kept_ref[:, s : s + 1]
+        tall += [jnp.where(kept, coeff_ref[s].astype(f32), 0.0)] * 2
     wide = jnp.dot(
         jnp.concatenate(tall, axis=0).astype(bf16), expand, preferred_element_type=f32
     )
@@ -79,7 +79,8 @@
     for s in range(slots):
         for t in range(columns // period):
             lanes = slice(t * period, (t + 1) * period)
-            piece = wide[s * rows : (s + 1) * rows, lanes]
+            piece = wide[s * 2 * PARTS : (s + 1) * 2 * PARTS, lanes]
+            piece = jnp.concatenate([piece] * (rows // (2 * PARTS)), axis=0)
             out_ref[s, :, lanes] = jnp.where(diagonal, piece, 0.0).astype(bf16)
 
 
@@ -89,12 +90,12 @@
     return pl.pallas_call(
         spread_kernel,
         out_shape=jax.ShapeDtypeStruct((slots, group * PARTS, modes * group), bf16),
-        in_specs=[SMEM, VMEM],
+        in_specs=[VMEM, VMEM],
         out_specs=VMEM,
         compiler_params=pltpu.CompilerParams(vmem_limit_bytes=SMALL),
-        cost_estimate=work(1.0),
+        cost_estimate=work(0.5),
         name="spread_stage",
-    )(kept, coeffs)
+    )(kept[None], coeffs)
 
 
 def kl_kernel(spread_ref, vectors_ref, keep_ref, send_ref, ready):
@@ -131,6 +132,26 @@
         cost_estimate=work(2.0),
         name="kl_stage",
     )(spread, vectors)
+
+
+def gather_kernel(own_ref, first_ref, middle_ref, given_ref, out_ref):
+    odd = lax.axis_index("freq") % 2 == 1
+    first, given = first_ref[...], given_ref[...]
+    out_ref[0:1] = own_ref[...]
+    out_ref[1:2] = jnp.where(odd, given, first)
+    out_ref[2:3] = middle_ref[...]
+    out_ref[3:4] = jnp.where(odd, first, given)
+
+
+def gather(*rows):
+    return pl.pallas_call(
+        gather_kernel,
+        out_shape=jax.ShapeDtypeStruct((4, rows[0].shape[1]), rows[0].dtype),
+        in_specs=[VMEM] * 4,
+        out_specs=VMEM,
+        compiler_params=pltpu.CompilerParams(vmem_limit_bytes=SMALL),
+        name="gather",
+    )(*rows)
 
 
 def fold_kernel(bit, held_ref, got_ref, keep_ref, send_ref):
@@ -361,7 +382,7 @@
             pltpu.VMEM((width // LANES, BLOCKS * STEPS, LANES), f32),
         ],
         compiler_params=pltpu.CompilerParams(vmem_limit_bytes=LIMIT),
-        cost_estimate=work(2.0),
+        cost_estimate=work(4.0),
         name="legendre_stage",
     )(ids)
 
@@ -503,11 +524,22 @@
 def local(members, pieces, m_table, retained_modes, cycle_ids, kl_coeffs, kl_vectors, beam_matrix):
     slots, share = beam_matrix.shape[:2]
     ids = lead(jnp.concatenate([m_table, cycle_ids])[None])
-    bit = 1
-    while bit < members:
-        far = swap(ids, "ma", members, bit)
-        ids = stack(ids, far)
-        bit *= 2
+    if members == 4:
+        pairs = [
+            (a * pieces + k, (a ^ (3 if k % 2 else 1)) * pieces + k)
+            for a in range(members)
+            for k in range(pieces)
+        ]
+        first = lax.ppermute(ids, ("ma", "freq"), pairs)
+        middle = swap(ids, "ma", members, 2)
+        given = swap(first, "freq", pieces, 1)
+        ids = gather(ids, first, middle, given)
+    else:
+        bit = 1
+        while bit < members:
+            far = swap(ids, "ma", members, bit)
+            ids = stack(ids, far)
+            bit *= 2
     spread = spread_stage(retained_modes, kl_coeffs, kl_vectors.shape[2])
     held, send = kl_stage(spread, kl_vectors, pieces)
     bit = 1

time: 32.3 us -> 29.9 us (0.926)
  starting transfers between devices: 14.3 us -> 12.5 us
  Pallas kernels: 6.87 us -> 6.37 us
    ppermute x8, starting transfers between devices: 14.3 us -> 11 us  [swap(): return lax.ppermute(value, axis, [(k, k ^ bit) for k in range(size)])]
    ppermute x8, waiting for transfers between devices: 7.28 us -> 5.1 us  [swap(): return lax.ppermute(value, axis, [(k, k ^ bit) for k in range(size)])]
    ppermute x0 -> x1, waiting for transfers between devices: none -> 2.08 us  [local(): first = lax.ppermute(ids, ('ma', 'freq'), pairs)]
    ppermute x0 -> x1, starting transfers between devices: none -> 1.49 us  [local(): first = lax.ppermute(ids, ('ma', 'freq'), pairs)]
    pallas_call x1, Pallas kernels: 0.75 us -> 0.22 us  [spread_stage(): pl.pallas_call(spread_kernel, out_shape=jax.ShapeDtypeStruct((slots, grou...]
  transfers between devices with their start and end apart: 8 -> 9, of which waited for: 6 -> 6; matrix products, arithmetic and copies ran while one was open for 0% -> 0% of each run, Pallas kernels for 13% -> 14%
where the time goes in v5:
time: 29.9 us; the launch traced here: 29.7 us
  starting transfers between devices  12.5 us (42%)
  waiting for transfers between devices  7.18 us (24%)
  Pallas kernels  6.37 us (21%)
  local copies, waits for them, and re-layouts  3.57 us (12%)
    ppermute x8, starting transfers between devices, swap(): return lax.ppermute(value, axis, [(k, k ^ bit) for k in range(size)])  11 us
    ppermute x8, waiting for transfers between devices, swap(): return lax.ppermute(value, axis, [(k, k ^ bit) for k in range(size)])  5.1 us
    unnamed x14, local copies, waits for them, and re-layouts  3.57 us
    ppermute x1, waiting for transfers between devices, local(): first = lax.ppermute(ids, ('ma', 'freq'), pairs)  2.08 us
    pallas_call x1, Pallas kernels, projection(): pl.pallas_call(projection_kernel, out_shape=jax.ShapeDtypeStruct((slots,...  1.67 us
    pallas_call x1, Pallas kernels, legendre_stage(): pl.pallas_call(functools.partial(legendre_kernel, slots), out_shape=jax.S...  1.56 us
    ppermute x1, starting transfers between devices, local(): first = lax.ppermute(ids, ('ma', 'freq'), pairs)  1.49 us
    pallas_call x1, Pallas kernels, sky_maps(): pl.pallas_call(functools.partial(sky_kernel, members), out_shape=jax.Shap...  0.98 us
  transfers between devices with their start and end apart: 9, of which 6 were waited for; matrix products, arithmetic and copies ran while one was open for 0% of the time, Pallas kernels for 14%

profile of v5, /device:TPU:0, one launch (start us, length us, event | category | flops | bytes accessed | tf_op | source)
XLA Modules:
  0.0 29.7 jit_solution(12818645063753683202)
XLA Ops:
  0.0 0.7 %copy-done.1 = bf16[2,4,64]{2,1,0:T(4,128)(2,1)S(1)} copy-done((bf16[2,4,64]{2,1,0:T(4,128)(2,1)S(1)}, bf16[2,4,64]{2,1,0:T(4,128)(2,1)}, u32[]{:S(2)}) %copy-start.1) | copy-done | bytes 1048
  0.7 0.7 %copy-done.2 = s32[2]{0:T(128)S(1)} copy-done((s32[2]{0:T(128)S(1)}, s32[2]{0:T(128)}, u32[]{:S(2)}) %copy-start.2) | copy-done | bytes 32
  1.4 0.2 spread_stage.1.spread_ref
  1.6 0.0 copy-start
  1.6 2.2 %copy-done = bf16[2,64,32,512]{3,2,1,0:T(8,128)(2,1)S(1)} copy-done((bf16[2,64,32,512]{3,2,1,0:T(8,128)(2,1)S(1)}, bf16[2,64,32,512]{3,2,1,0:T(8,128)(2,1)}, u32[]{:S(2)}) %copy-start) | copy-done | bytes 4194328
  3.8 0.9 %kl_stage.1 = (f32[4,2,16,512]{3,2,1,0:T(8,128)S(1)}, bf16[4,2,16,512]{3,2,1,0:T(8,128)(2,1)S(1)}) custom-call(bf16[2,64,1024]{2,1,0:T(8,128)(2,1)S(1)} %spread_stage.1.spread_ref, bf16[2,64,32,512]{3,2,1,0:T(8,128)(2,1)S(1)} %copy-done), custom_call_target="tpu_custom_call" | custom-call | flops 2000000000 | bytes 4096 | tf_op jit(solution)/shard_map/kl_stage/pallas_call | solution.py:125
  4.7 0.6 %collective-permute-start = (bf16[4,2,16,512]{3,2,1,0:T(8,128)(2,1)S(1)}, bf16[4,2,16,512]{3,2,1,0:T(8,128)(2,1)S(1)}, u32[]{:S(2)}, u32[]{:S(2)}) collective-permute-start(bf16[4,2,16,512]{3,2,1,0:T(8,128)(2,1)S(1)} %get-tuple-element.16), channel_id=1, source_target_pairs={{0,1},{1,0},{2,3},{3,2},{4,5},{5,4},{6,7},{7,6},{8,9},{9,8},{10,11... | collective-permute-start | bytes 393224 | tf_op jit(solution)/shard_map/ppermute | solution.py:521
  5.2 0.0 copy-done.4
  5.2 0.1 add_bitcast_fusion.in_ref
  5.3 2.6 %collective-permute-start.4 = (s32[1,10]{1,0:T(1,128)S(1)}, s32[1,10]{1,0:T(1,128)S(1)}, u32[]{:S(2)}, u32[]{:S(2)}) collective-permute-start(s32[1,10]{1,0:T(1,128)S(1)} %lead.1.own_ref), channel_id=1, source_target_pairs={{0,16},{8,24},{16,0},{24,8},{1,17},{9,25},{17,1},{25,9},{2,18},{10... | collective-permute-start | bytes 128 | tf_op jit(solution)/shard_map/ppermute | solution.py:521
  7.9 1.5 %collective-permute-start.3 = (s32[1,10]{1,0:T(1,128)S(1)}, s32[1,10]{1,0:T(1,128)S(1)}, u32[]{:S(2)}, u32[]{:S(2)}) collective-permute-start(s32[1,10]{1,0:T(1,128)S(1)} %lead.1.own_ref), channel_id=1, source_target_pairs={{0,8},{1,25},{2,10},{3,27},{4,12},{5,29},{6,14},{7,31},{8,0},{9,17... | collective-permute-start | bytes 128 | tf_op jit(solution)/shard_map/ppermute | solution.py:533
  9.3 2.1 %collective-permute-done.3.first_ref = s32[1,10]{1,0:T(1,128)S(1)} collective-permute-done((s32[1,10]{1,0:T(1,128)S(1)}, s32[1,10]{1,0:T(1,128)S(1)}, u32[]{:S(2)}, u32[]{:S(2)}) %collective-permute-start.3) | collective-permute-done | bytes 72 | tf_op jit(solution)/shard_map/ppermute | solution.py:533
  11.4 0.0 collective-permute-start.5
  11.4 0.0 collective-permute-done.4.middle_ref
  11.4 1.2 %collective-permute-done.5.given_ref = s32[1,10]{1,0:T(1,128)S(1)} collective-permute-done((s32[1,10]{1,0:T(1,128)S(1)}, s32[1,10]{1,0:T(1,128)S(1)}, u32[]{:S(2)}, u32[]{:S(2)}) %collective-permute-start.5) | collective-permute-done | bytes 72 | tf_op jit(solution)/shard_map/ppermute | solution.py:521
  12.6 0.0 collective-permute-done.got_ref
  12.6 0.0 slice-start.1
  12.7 1.6 %collective-permute-start.1 = (bf16[2,2,16,512]{3,2,1,0:T(8,128)(2,1)S(1)}, bf16[2,2,16,512]{3,2,1,0:T(8,128)(2,1)S(1)}, u32[]{:S(2)}, u32[]{:S(2)}) collective-permute-start(bf16[2,2,16,512]{3,2,1,0:T(8,128)(2,1)S(1)} %get-tuple-element.18), channel_id=1, source_target_pairs={{0,2},{1,3},{2,0},{3,1},{4,6},{5,7},{6,4},{7,5},{8,10},{9,11},{10,... | collective-permute-start | bytes 196616 | tf_op jit(solution)/shard_map/ppermute | solution.py:521
  14.3 1.6 %legendre_stage.1.turned_ref = bf16[128,1024]{1,0:T(8,128)(2,1)S(1)} custom-call(s32[4,10]{1,0:T(4,128)S(1)} %gather.1.ids_ref), custom_call_target="tpu_custom_call" | custom-call | flops 4000000000 | bytes 4096 | tf_op jit(solution)/shard_map/legendre_stage/pallas_call | solution.py:371
  15.9 1.1 %collective-permute-done.1.got_ref = bf16[2,2,16,512]{3,2,1,0:T(8,128)(2,1)S(1)} collective-permute-done((bf16[2,2,16,512]{3,2,1,0:T(8,128)(2,1)S(1)}, bf16[2,2,16,512]{3,2,1,0:T(8,128)(2,1)S(1)}, u32[]{:S(2)}, u32[]{:S(2)}) %collective-permute-start.1) | collective-permute-done | bytes 65568 | tf_op jit(solution)/shard_map/ppermute | solution.py:521
  17.0 2.7 %collective-permute-start.2 = (bf16[1,2,16,512]{3,2,1,0:T(8,128)(2,1)S(1)}, bf16[1,2,16,512]{3,2,1,0:T(8,128)(2,1)S(1)}, u32[]{:S(2)}, u32[]{:S(2)}) collective-permute-start(bf16[1,2,16,512]{3,2,1,0:T(8,128)(2,1)S(1)} %get-tuple-element.20), channel_id=1, source_target_pairs={{0,4},{1,5},{2,6},{3,7},{4,0},{5,1},{6,2},{7,3},{8,12},{9,13},{10,... | collective-permute-start | bytes 98312 | tf_op jit(solution)/shard_map/ppermute | solution.py:521
  19.7 1.7 %projection.1.folded_ref = bf16[2,128,512]{2,1,0:T(8,128)(2,1)S(1)} custom-call(s32[4,10]{1,0:T(4,128)S(1)} %gather.1.ids_ref, bf16[128,1024]{1,0:T(8,128)(2,1)S(1)} %legendre_stage.1.turned_ref, bf16[2,4,1024,512]{3,2,1,0:T(8,128)(2,1)S(1)} %bitcast.4), custom_call_target="tpu_custom_call" | custom-call | flops 2000000000 | bytes 4096 | tf_op jit(solution)/shard_map/projection/pallas_call | solution.py:425
  21.3 0.5 %collective-permute-done.2.got_ref = bf16[1,2,16,512]{3,2,1,0:T(8,128)(2,1)S(1)} collective-permute-done((bf16[1,2,16,512]{3,2,1,0:T(8,128)(2,1)S(1)}, bf16[1,2,16,512]{3,2,1,0:T(8,128)(2,1)S(1)}, u32[]{:S(2)}, u32[]{:S(2)}) %collective-permute-start.2) | collective-permute-done | bytes 32800 | tf_op jit(solution)/shard_map/ppermute | solution.py:521
  21.9 0.2 cycle_values.1
  22.1 1.6 %collective-permute-start.6 = (bf16[32,128]{1,0:T(8,128)(2,1)S(1)}, bf16[32,128]{1,0:T(8,128)(2,1)S(1)}, u32[]{:S(2)}, u32[]{:S(2)}) collective-permute-start(bf16[32,128]{1,0:T(8,128)(2,1)S(1)} %get-tuple-element.22), channel_id=1, source_target_pairs={{0,8},{8,0},{16,24},{24,16},{1,9},{9,1},{17,25},{25,17},{2,10},{10... | collective-permute-start | bytes 24584 | tf_op jit(solution)/shard_map/ppermute | solution.py:521
  23.7 0.5 %collective-permute-start.7 = (bf16[32,128]{1,0:T(8,128)(2,1)S(1)}, bf16[32,128]{1,0:T(8,128)(2,1)S(1)}, u32[]{:S(2)}, u32[]{:S(2)}) collective-permute-start(bf16[32,128]{1,0:T(8,128)(2,1)S(1)} %get-tuple-element.23), channel_id=1, source_target_pairs={{0,16},{8,24},{16,0},{24,8},{1,17},{9,25},{17,1},{25,9},{2,18},{10... | collective-permute-start | bytes 24584 | tf_op jit(solution)/shard_map/ppermute | solution.py:521
  24.2 1.5 %collective-permute-start.8 = (bf16[32,128]{1,0:T(8,128)(2,1)S(1)}, bf16[32,128]{1,0:T(8,128)(2,1)S(1)}, u32[]{:S(2)}, u32[]{:S(2)}) collective-permute-start(bf16[32,128]{1,0:T(8,128)(2,1)S(1)} %get-tuple-element.24), channel_id=1, source_target_pairs={{0,24},{8,16},{16,8},{24,0},{1,25},{9,17},{17,9},{25,1},{2,26},{10... | collective-permute-start | bytes 24584 | tf_op jit(solution)/shard_map/ppermute | solution.py:521
  25.7 0.8 %fourier_stage.1.refs_4_ = bf16[128,2048]{1,0:T(8,128)(2,1)S(1)} custom-call(s32[4,10]{1,0:T(4,128)S(1)} %gather.1.ids_ref), custom_call_target="tpu_custom_call" | custom-call | flops 500000000 | bytes 4096 | tf_op jit(solution)/shard_map/fourier_stage/pallas_call | solution.py:357
  26.5 0.0 collective-permute-done.6.refs_1_
  26.5 0.9 %collective-permute-done.7.refs_2_ = bf16[32,128]{1,0:T(8,128)(2,1)S(1)} collective-permute-done((bf16[32,128]{1,0:T(8,128)(2,1)S(1)}, bf16[32,128]{1,0:T(8,128)(2,1)S(1)}, u32[]{:S(2)}, u32[]{:S(2)}) %collective-permute-start.7) | collective-permute-done | bytes 8224 | tf_op jit(solution)/shard_map/ppermute | solution.py:521
  27.3 1.4 %collective-permute-done.8.refs_3_ = bf16[32,128]{1,0:T(8,128)(2,1)S(1)} collective-permute-done((bf16[32,128]{1,0:T(8,128)(2,1)S(1)}, bf16[32,128]{1,0:T(8,128)(2,1)S(1)}, u32[]{:S(2)}, u32[]{:S(2)}) %collective-permute-start.8) | collective-permute-done | bytes 8224 | tf_op jit(solution)/shard_map/ppermute | solution.py:521
  28.8 1.0 %sky_maps.1 = f32[8,2,4,2048]{3,2,1,0:T(4,128)} custom-call(bf16[32,128]{1,0:T(8,128)(2,1)S(1)} %get-tuple-element.21.refs_0_, bf16[32,128]{1,0:T(8,128)(2,1)S(1)} %collective-permute-done.6.refs_1_, bf16[32,128]{1,0:T(8,128)(2,1)S(1)} %collective-permute-done.7.refs_2_, bf16[32,128]{1,0:T(8,128)(2,1)S(1)} %collective-permute-done.8.refs_3_, ...), custom_call_target="tpu_custom_call" | custom-call | tf_op jit(solution)/shard_map/sky_maps/pallas_call | solution.py:509
  (13 shorter events, 0.1 us)
Async XLA Ops:
  0.0 5.2 %copy-start.3 = (s32[8]{0:T(128)S(1)}, s32[8]{0:T(128)}, u32[]{:S(2)}) copy-start(s32[8]{0:T(128)} %param.8) | copy-start | bytes 100
  0.0 5.2 %copy-start.4 = (s32[2]{0:T(128)S(1)}, s32[2]{0:T(128)}, u32[]{:S(2)}) copy-start(s32[2]{0:T(128)} %param.6) | copy-start | bytes 28
  0.0 0.7 %copy-start.1 = (bf16[2,4,64]{2,1,0:T(4,128)(2,1)S(1)}, bf16[2,4,64]{2,1,0:T(4,128)(2,1)}, u32[]{:S(2)}) copy-start(bf16[2,4,64]{2,1,0:T(4,128)(2,1)} %coeff_ref.1) | copy-start | bytes 3076
  0.7 0.7 %copy-start.2 = (s32[2]{0:T(128)S(1)}, s32[2]{0:T(128)}, u32[]{:S(2)}) copy-start(s32[2]{0:T(128)} %param.7) | copy-start | bytes 28
  1.6 2.2 %copy-start = (bf16[2,64,32,512]{3,2,1,0:T(8,128)(2,1)S(1)}, bf16[2,64,32,512]{3,2,1,0:T(8,128)(2,1)}, u32[]{:S(2)}) copy-start(bf16[2,64,32,512]{3,2,1,0:T(8,128)(2,1)} %vectors_ref.1) | copy-start | bytes 12582916
  4.7 7.9 %collective-permute-start = (bf16[4,2,16,512]{3,2,1,0:T(8,128)(2,1)S(1)}, bf16[4,2,16,512]{3,2,1,0:T(8,128)(2,1)S(1)}, u32[]{:S(2)}, u32[]{:S(2)}) collective-permute-start(bf16[4,2,16,512]{3,2,1,0:T(8,128)(2,1)S(1)} %get-tuple-element.16), channel_id=1, source_target_pairs={{0,1},{1,0},{2,3},{3,2},{4,5},{5,4},{6,7},{7,6},{8,9},{9,8},{10,11... | collective-permute-start | bytes 393224 | tf_op jit(solution)/shard_map/ppermute | solution.py:521
  5.3 14.4 %slice-start = ((s8[8388608]{0:T(1024)(128)(4,1)}), s8[4194304]{0:T(1024)(128)(4,1)S(1)}, s32[]{:S(2)}) async-start(s8[8388608]{0:T(1024)(128)(4,1)} %bitcast.3), calls=%async_computation | async-start | bytes 8388608
  5.3 6.1 %collective-permute-start.4 = (s32[1,10]{1,0:T(1,128)S(1)}, s32[1,10]{1,0:T(1,128)S(1)}, u32[]{:S(2)}, u32[]{:S(2)}) collective-permute-start(s32[1,10]{1,0:T(1,128)S(1)} %lead.1.own_ref), channel_id=1, source_target_pairs={{0,16},{8,24},{16,0},{24,8},{1,17},{9,25},{17,1},{25,9},{2,18},{10... | collective-permute-start | bytes 128 | tf_op jit(solution)/shard_map/ppermute | solution.py:521
  7.9 3.6 %collective-permute-start.3 = (s32[1,10]{1,0:T(1,128)S(1)}, s32[1,10]{1,0:T(1,128)S(1)}, u32[]{:S(2)}, u32[]{:S(2)}) collective-permute-start(s32[1,10]{1,0:T(1,128)S(1)} %lead.1.own_ref), channel_id=1, source_target_pairs={{0,8},{1,25},{2,10},{3,27},{4,12},{5,29},{6,14},{7,31},{8,0},{9,17... | collective-permute-start | bytes 128 | tf_op jit(solution)/shard_map/ppermute | solution.py:533
  11.4 1.2 %collective-permute-start.5 = (s32[1,10]{1,0:T(1,128)S(1)}, s32[1,10]{1,0:T(1,128)S(1)}, u32[]{:S(2)}, u32[]{:S(2)}) collective-permute-start(s32[1,10]{1,0:T(1,128)S(1)} %collective-permute-done.3.first_ref), channel_id=1, source_target_pairs={{0,1},{1,0},{2,3},{3,2},{4,5},{5,4},{6,7},{7,6},{8,9},{9,8},{10,11... | collective-permute-start | bytes 128 | tf_op jit(solution)/shard_map/ppermute | solution.py:521
  12.6 7.0 %slice-start.1 = ((s8[8388608]{0:T(1024)(128)(4,1)}), s8[4194304]{0:T(1024)(128)(4,1)S(1)}, s32[]{:S(2)}) async-start(s8[8388608]{0:T(1024)(128)(4,1)} %bitcast.3), calls=%async_computation.1 | async-start | bytes 8388608
  12.7 4.3 %collective-permute-start.1 = (bf16[2,2,16,512]{3,2,1,0:T(8,128)(2,1)S(1)}, bf16[2,2,16,512]{3,2,1,0:T(8,128)(2,1)S(1)}, u32[]{:S(2)}, u32[]{:S(2)}) collective-permute-start(bf16[2,2,16,512]{3,2,1,0:T(8,128)(2,1)S(1)} %get-tuple-element.18), channel_id=1, source_target_pairs={{0,2},{1,3},{2,0},{3,1},{4,6},{5,7},{6,4},{7,5},{8,10},{9,11},{10,... | collective-permute-start | bytes 196616 | tf_op jit(solution)/shard_map/ppermute | solution.py:521
  17.0 4.9 %collective-permute-start.2 = (bf16[1,2,16,512]{3,2,1,0:T(8,128)(2,1)S(1)}, bf16[1,2,16,512]{3,2,1,0:T(8,128)(2,1)S(1)}, u32[]{:S(2)}, u32[]{:S(2)}) collective-permute-start(bf16[1,2,16,512]{3,2,1,0:T(8,128)(2,1)S(1)} %get-tuple-element.20), channel_id=1, source_target_pairs={{0,4},{1,5},{2,6},{3,7},{4,0},{5,1},{6,2},{7,3},{8,12},{9,13},{10,... | collective-permute-start | bytes 98312 | tf_op jit(solution)/shard_map/ppermute | solution.py:521
  22.1 4.3 %collective-permute-start.6 = (bf16[32,128]{1,0:T(8,128)(2,1)S(1)}, bf16[32,128]{1,0:T(8,128)(2,1)S(1)}, u32[]{:S(2)}, u32[]{:S(2)}) collective-permute-start(bf16[32,128]{1,0:T(8,128)(2,1)S(1)} %get-tuple-element.22), channel_id=1, source_target_pairs={{0,8},{8,0},{16,24},{24,16},{1,9},{9,1},{17,25},{25,17},{2,10},{10... | collective-permute-start | bytes 24584 | tf_op jit(solution)/shard_map/ppermute | solution.py:521
  23.7 3.7 %collective-permute-start.7 = (bf16[32,128]{1,0:T(8,128)(2,1)S(1)}, bf16[32,128]{1,0:T(8,128)(2,1)S(1)}, u32[]{:S(2)}, u32[]{:S(2)}) collective-permute-start(bf16[32,128]{1,0:T(8,128)(2,1)S(1)} %get-tuple-element.23), channel_id=1, source_target_pairs={{0,16},{8,24},{16,0},{24,8},{1,17},{9,25},{17,1},{25,9},{2,18},{10... | collective-permute-start | bytes 24584 | tf_op jit(solution)/shard_map/ppermute | solution.py:521
  24.2 4.5 %collective-permute-start.8 = (bf16[32,128]{1,0:T(8,128)(2,1)S(1)}, bf16[32,128]{1,0:T(8,128)(2,1)S(1)}, u32[]{:S(2)}, u32[]{:S(2)}) collective-permute-start(bf16[32,128]{1,0:T(8,128)(2,1)S(1)} %get-tuple-element.24), channel_id=1, source_target_pairs={{0,24},{8,16},{16,8},{24,0},{1,25},{9,17},{17,9},{25,1},{2,26},{10... | collective-permute-start | bytes 24584 | tf_op jit(solution)/shard_map/ppermute | solution.py:521

commit v6 on v5

--- a/solution.py
+++ b/solution.py
@@ -98,25 +98,25 @@
     )(kept[None], coeffs)
 
 
-def kl_kernel(spread_ref, vectors_ref, keep_ref, send_ref, ready):
+def kl_kernel(spread_ref, vectors_ref, keep_ref, send_ref):
     slots, modes, channels, depth = vectors_ref.shape
     group = spread_ref.shape[1] // PARTS
     pieces = keep_ref.shape[0] * 2
     share = channels // pieces
-    parity = lax.axis_index("freq") % 2
+    rows = share * PARTS
+    even = lax.axis_index("freq") % 2 == 0
     for s in range(slots):
         for g in range(channels // group):
             block = vectors_ref[s, :, g * group : (g + 1) * group, :]
             sums = jnp.dot(
                 spread_ref[s], block.reshape(modes * group, depth), preferred_element_type=f32
             )
-            for i in range(group // share):
-                piece = g * (group // share) + i
-                ready[(piece + parity) % 2, piece // 2, s] = sums[
-                    i * share * PARTS : (i + 1) * share * PARTS
-                ]
-    keep_ref[...] = ready[0]
-    send_ref[...] = ready[1].astype(bf16)
+            for i in range(group // share // 2):
+                pair = g * (group // share // 2) + i
+                first = sums[2 * i * rows : (2 * i + 1) * rows]
+                second = sums[(2 * i + 1) * rows : (2 * i + 2) * rows]
+                keep_ref[pair, s] = jnp.where(even, first, second)
+                send_ref[pair, s] = jnp.where(even, second, first).astype(bf16)
 
 
 def kl_stage(spread, vectors, pieces):
@@ -127,7 +127,6 @@
         out_shape=(jax.ShapeDtypeStruct(shape, f32), jax.ShapeDtypeStruct(shape, bf16)),
         in_specs=[VMEM, VMEM],
         out_specs=(VMEM, VMEM),
-        scratch_shapes=[pltpu.VMEM((2, *shape), f32)],
         compiler_params=pltpu.CompilerParams(vmem_limit_bytes=LIMIT),
         cost_estimate=work(2.0),
         name="kl_stage",

time: 29.9 us -> 29.9 us (level)
  no operation moved by 1% of the time
where the time goes in v6:
time: 29.9 us; the launch traced here: 29.7 us
  starting transfers between devices  12.5 us (42%)
  waiting for transfers between devices  7.17 us (24%)
  Pallas kernels  6.34 us (21%)
  local copies, waits for them, and re-layouts  3.57 us (12%)
    ppermute x8, starting transfers between devices, swap(): return lax.ppermute(value, axis, [(k, k ^ bit) for k in range(size)])  11 us
    ppermute x8, waiting for transfers between devices, swap(): return lax.ppermute(value, axis, [(k, k ^ bit) for k in range(size)])  5.09 us
    unnamed x14, local copies, waits for them, and re-layouts  3.57 us
    ppermute x1, waiting for transfers between devices, local(): first = lax.ppermute(ids, ('ma', 'freq'), pairs)  2.08 us
    pallas_call x1, Pallas kernels, projection(): pl.pallas_call(projection_kernel, out_shape=jax.ShapeDtypeStruct((slots,...  1.67 us
    pallas_call x1, Pallas kernels, legendre_stage(): pl.pallas_call(functools.partial(legendre_kernel, slots), out_shape=jax.S...  1.56 us
    ppermute x1, starting transfers between devices, local(): first = lax.ppermute(ids, ('ma', 'freq'), pairs)  1.49 us
    pallas_call x1, Pallas kernels, sky_maps(): pl.pallas_call(functools.partial(sky_kernel, members), out_shape=jax.Shap...  0.98 us
  transfers between devices with their start and end apart: 9, of which 6 were waited for; matrix products, arithmetic and copies ran while one was open for 0% of the time, Pallas kernels for 14%

profile of v6, /device:TPU:0, one launch (start us, length us, event | category | flops | bytes accessed | tf_op | source)
XLA Modules:
  0.0 29.7 jit_solution(1097574235773843042)
XLA Ops:
  0.0 0.7 %copy-done.1 = bf16[2,4,64]{2,1,0:T(4,128)(2,1)S(1)} copy-done((bf16[2,4,64]{2,1,0:T(4,128)(2,1)S(1)}, bf16[2,4,64]{2,1,0:T(4,128)(2,1)}, u32[]{:S(2)}) %copy-start.1) | copy-done | bytes 1048
  0.7 0.7 %copy-done.2 = s32[2]{0:T(128)S(1)} copy-done((s32[2]{0:T(128)S(1)}, s32[2]{0:T(128)}, u32[]{:S(2)}) %copy-start.2) | copy-done | bytes 32
  1.4 0.2 spread_stage.1.spread_ref
  1.6 0.0 copy-start
  1.6 2.2 %copy-done = bf16[2,64,32,512]{3,2,1,0:T(8,128)(2,1)S(1)} copy-done((bf16[2,64,32,512]{3,2,1,0:T(8,128)(2,1)S(1)}, bf16[2,64,32,512]{3,2,1,0:T(8,128)(2,1)}, u32[]{:S(2)}) %copy-start) | copy-done | bytes 4194328
  3.8 0.8 %kl_stage.1 = (f32[4,2,16,512]{3,2,1,0:T(8,128)S(1)}, bf16[4,2,16,512]{3,2,1,0:T(8,128)(2,1)S(1)}) custom-call(bf16[2,64,1024]{2,1,0:T(8,128)(2,1)S(1)} %spread_stage.1.spread_ref, bf16[2,64,32,512]{3,2,1,0:T(8,128)(2,1)S(1)} %copy-done), custom_call_target="tpu_custom_call" | custom-call | flops 2000000000 | bytes 4096 | tf_op jit(solution)/shard_map/kl_stage/pallas_call | solution.py:125
  4.6 0.6 %collective-permute-start = (bf16[4,2,16,512]{3,2,1,0:T(8,128)(2,1)S(1)}, bf16[4,2,16,512]{3,2,1,0:T(8,128)(2,1)S(1)}, u32[]{:S(2)}, u32[]{:S(2)}) collective-permute-start(bf16[4,2,16,512]{3,2,1,0:T(8,128)(2,1)S(1)} %get-tuple-element.16), channel_id=1, source_target_pairs={{0,1},{1,0},{2,3},{3,2},{4,5},{5,4},{6,7},{7,6},{8,9},{9,8},{10,11... | collective-permute-start | bytes 393224 | tf_op jit(solution)/shard_map/ppermute | solution.py:520
  5.2 0.1 add_bitcast_fusion.in_ref
  5.3 2.6 %collective-permute-start.4 = (s32[1,10]{1,0:T(1,128)S(1)}, s32[1,10]{1,0:T(1,128)S(1)}, u32[]{:S(2)}, u32[]{:S(2)}) collective-permute-start(s32[1,10]{1,0:T(1,128)S(1)} %lead.1.own_ref), channel_id=1, source_target_pairs={{0,16},{8,24},{16,0},{24,8},{1,17},{9,25},{17,1},{25,9},{2,18},{10... | collective-permute-start | bytes 128 | tf_op jit(solution)/shard_map/ppermute | solution.py:520
  7.8 1.5 %collective-permute-start.3 = (s32[1,10]{1,0:T(1,128)S(1)}, s32[1,10]{1,0:T(1,128)S(1)}, u32[]{:S(2)}, u32[]{:S(2)}) collective-permute-start(s32[1,10]{1,0:T(1,128)S(1)} %lead.1.own_ref), channel_id=1, source_target_pairs={{0,8},{1,25},{2,10},{3,27},{4,12},{5,29},{6,14},{7,31},{8,0},{9,17... | collective-permute-start | bytes 128 | tf_op jit(solution)/shard_map/ppermute | solution.py:532
  9.3 2.1 %collective-permute-done.3.first_ref = s32[1,10]{1,0:T(1,128)S(1)} collective-permute-done((s32[1,10]{1,0:T(1,128)S(1)}, s32[1,10]{1,0:T(1,128)S(1)}, u32[]{:S(2)}, u32[]{:S(2)}) %collective-permute-start.3) | collective-permute-done | bytes 72 | tf_op jit(solution)/shard_map/ppermute | solution.py:532
  11.4 0.0 collective-permute-start.5
  11.4 0.0 collective-permute-done.4.middle_ref
  11.4 1.2 %collective-permute-done.5.given_ref = s32[1,10]{1,0:T(1,128)S(1)} collective-permute-done((s32[1,10]{1,0:T(1,128)S(1)}, s32[1,10]{1,0:T(1,128)S(1)}, u32[]{:S(2)}, u32[]{:S(2)}) %collective-permute-start.5) | collective-permute-done | bytes 72 | tf_op jit(solution)/shard_map/ppermute | solution.py:520
  12.6 0.0 collective-permute-done.got_ref
  12.6 0.0 slice-start.1
  12.6 1.6 %collective-permute-start.1 = (bf16[2,2,16,512]{3,2,1,0:T(8,128)(2,1)S(1)}, bf16[2,2,16,512]{3,2,1,0:T(8,128)(2,1)S(1)}, u32[]{:S(2)}, u32[]{:S(2)}) collective-permute-start(bf16[2,2,16,512]{3,2,1,0:T(8,128)(2,1)S(1)} %get-tuple-element.18), channel_id=1, source_target_pairs={{0,2},{1,3},{2,0},{3,1},{4,6},{5,7},{6,4},{7,5},{8,10},{9,11},{10,... | collective-permute-start | bytes 196616 | tf_op jit(solution)/shard_map/ppermute | solution.py:520
  14.3 1.6 %legendre_stage.1.turned_ref = bf16[128,1024]{1,0:T(8,128)(2,1)S(1)} custom-call(s32[4,10]{1,0:T(4,128)S(1)} %gather.1.ids_ref), custom_call_target="tpu_custom_call" | custom-call | flops 4000000000 | bytes 4096 | tf_op jit(solution)/shard_map/legendre_stage/pallas_call | solution.py:370
  15.8 1.1 %collective-permute-done.1.got_ref = bf16[2,2,16,512]{3,2,1,0:T(8,128)(2,1)S(1)} collective-permute-done((bf16[2,2,16,512]{3,2,1,0:T(8,128)(2,1)S(1)}, bf16[2,2,16,512]{3,2,1,0:T(8,128)(2,1)S(1)}, u32[]{:S(2)}, u32[]{:S(2)}) %collective-permute-start.1) | collective-permute-done | bytes 65568 | tf_op jit(solution)/shard_map/ppermute | solution.py:520
  17.0 2.7 %collective-permute-start.2 = (bf16[1,2,16,512]{3,2,1,0:T(8,128)(2,1)S(1)}, bf16[1,2,16,512]{3,2,1,0:T(8,128)(2,1)S(1)}, u32[]{:S(2)}, u32[]{:S(2)}) collective-permute-start(bf16[1,2,16,512]{3,2,1,0:T(8,128)(2,1)S(1)} %get-tuple-element.20), channel_id=1, source_target_pairs={{0,4},{1,5},{2,6},{3,7},{4,0},{5,1},{6,2},{7,3},{8,12},{9,13},{10,... | collective-permute-start | bytes 98312 | tf_op jit(solution)/shard_map/ppermute | solution.py:520
  19.7 0.0 slice-done.1
  19.7 1.7 %projection.1.folded_ref = bf16[2,128,512]{2,1,0:T(8,128)(2,1)S(1)} custom-call(s32[4,10]{1,0:T(4,128)S(1)} %gather.1.ids_ref, bf16[128,1024]{1,0:T(8,128)(2,1)S(1)} %legendre_stage.1.turned_ref, bf16[2,4,1024,512]{3,2,1,0:T(8,128)(2,1)S(1)} %bitcast.4), custom_call_target="tpu_custom_call" | custom-call | flops 2000000000 | bytes 4096 | tf_op jit(solution)/shard_map/projection/pallas_call | solution.py:424
  21.3 0.5 %collective-permute-done.2.got_ref = bf16[1,2,16,512]{3,2,1,0:T(8,128)(2,1)S(1)} collective-permute-done((bf16[1,2,16,512]{3,2,1,0:T(8,128)(2,1)S(1)}, bf16[1,2,16,512]{3,2,1,0:T(8,128)(2,1)S(1)}, u32[]{:S(2)}, u32[]{:S(2)}) %collective-permute-start.2) | collective-permute-done | bytes 32800 | tf_op jit(solution)/shard_map/ppermute | solution.py:520
  21.9 0.2 cycle_values.1
  22.1 1.6 %collective-permute-start.6 = (bf16[32,128]{1,0:T(8,128)(2,1)S(1)}, bf16[32,128]{1,0:T(8,128)(2,1)S(1)}, u32[]{:S(2)}, u32[]{:S(2)}) collective-permute-start(bf16[32,128]{1,0:T(8,128)(2,1)S(1)} %get-tuple-element.22), channel_id=1, source_target_pairs={{0,8},{8,0},{16,24},{24,16},{1,9},{9,1},{17,25},{25,17},{2,10},{10... | collective-permute-start | bytes 24584 | tf_op jit(solution)/shard_map/ppermute | solution.py:520
  23.7 0.5 %collective-permute-start.7 = (bf16[32,128]{1,0:T(8,128)(2,1)S(1)}, bf16[32,128]{1,0:T(8,128)(2,1)S(1)}, u32[]{:S(2)}, u32[]{:S(2)}) collective-permute-start(bf16[32,128]{1,0:T(8,128)(2,1)S(1)} %get-tuple-element.23), channel_id=1, source_target_pairs={{0,16},{8,24},{16,0},{24,8},{1,17},{9,25},{17,1},{25,9},{2,18},{10... | collective-permute-start | bytes 24584 | tf_op jit(solution)/shard_map/ppermute | solution.py:520
  24.2 1.5 %collective-permute-start.8 = (bf16[32,128]{1,0:T(8,128)(2,1)S(1)}, bf16[32,128]{1,0:T(8,128)(2,1)S(1)}, u32[]{:S(2)}, u32[]{:S(2)}) collective-permute-start(bf16[32,128]{1,0:T(8,128)(2,1)S(1)} %get-tuple-element.24), channel_id=1, source_target_pairs={{0,24},{8,16},{16,8},{24,0},{1,25},{9,17},{17,9},{25,1},{2,26},{10... | collective-permute-start | bytes 24584 | tf_op jit(solution)/shard_map/ppermute | solution.py:520
  25.7 0.8 %fourier_stage.1.refs_4_ = bf16[128,2048]{1,0:T(8,128)(2,1)S(1)} custom-call(s32[4,10]{1,0:T(4,128)S(1)} %gather.1.ids_ref), custom_call_target="tpu_custom_call" | custom-call | flops 500000000 | bytes 4096 | tf_op jit(solution)/shard_map/fourier_stage/pallas_call | solution.py:356
  26.5 0.0 collective-permute-done.6.refs_1_
  26.5 0.9 %collective-permute-done.7.refs_2_ = bf16[32,128]{1,0:T(8,128)(2,1)S(1)} collective-permute-done((bf16[32,128]{1,0:T(8,128)(2,1)S(1)}, bf16[32,128]{1,0:T(8,128)(2,1)S(1)}, u32[]{:S(2)}, u32[]{:S(2)}) %collective-permute-start.7) | collective-permute-done | bytes 8224 | tf_op jit(solution)/shard_map/ppermute | solution.py:520
  27.3 1.4 %collective-permute-done.8.refs_3_ = bf16[32,128]{1,0:T(8,128)(2,1)S(1)} collective-permute-done((bf16[32,128]{1,0:T(8,128)(2,1)S(1)}, bf16[32,128]{1,0:T(8,128)(2,1)S(1)}, u32[]{:S(2)}, u32[]{:S(2)}) %collective-permute-start.8) | collective-permute-done | bytes 8224 | tf_op jit(solution)/shard_map/ppermute | solution.py:520
  28.7 1.0 %sky_maps.1 = f32[8,2,4,2048]{3,2,1,0:T(4,128)} custom-call(bf16[32,128]{1,0:T(8,128)(2,1)S(1)} %get-tuple-element.21.refs_0_, bf16[32,128]{1,0:T(8,128)(2,1)S(1)} %collective-permute-done.6.refs_1_, bf16[32,128]{1,0:T(8,128)(2,1)S(1)} %collective-permute-done.7.refs_2_, bf16[32,128]{1,0:T(8,128)(2,1)S(1)} %collective-permute-done.8.refs_3_, ...), custom_call_target="tpu_custom_call" | custom-call | tf_op jit(solution)/shard_map/sky_maps/pallas_call | solution.py:508
  (13 shorter events, 0.1 us)
Async XLA Ops:
  0.0 5.2 %copy-start.3 = (s32[8]{0:T(128)S(1)}, s32[8]{0:T(128)}, u32[]{:S(2)}) copy-start(s32[8]{0:T(128)} %param.8) | copy-start | bytes 100
  0.0 5.2 %copy-start.4 = (s32[2]{0:T(128)S(1)}, s32[2]{0:T(128)}, u32[]{:S(2)}) copy-start(s32[2]{0:T(128)} %param.6) | copy-start | bytes 28
  0.0 0.7 %copy-start.1 = (bf16[2,4,64]{2,1,0:T(4,128)(2,1)S(1)}, bf16[2,4,64]{2,1,0:T(4,128)(2,1)}, u32[]{:S(2)}) copy-start(bf16[2,4,64]{2,1,0:T(4,128)(2,1)} %coeff_ref.1) | copy-start | bytes 3076
  0.7 0.7 %copy-start.2 = (s32[2]{0:T(128)S(1)}, s32[2]{0:T(128)}, u32[]{:S(2)}) copy-start(s32[2]{0:T(128)} %param.7) | copy-start | bytes 28
  1.6 2.2 %copy-start = (bf16[2,64,32,512]{3,2,1,0:T(8,128)(2,1)S(1)}, bf16[2,64,32,512]{3,2,1,0:T(8,128)(2,1)}, u32[]{:S(2)}) copy-start(bf16[2,64,32,512]{3,2,1,0:T(8,128)(2,1)} %vectors_ref.1) | copy-start | bytes 12582916
  4.6 7.9 %collective-permute-start = (bf16[4,2,16,512]{3,2,1,0:T(8,128)(2,1)S(1)}, bf16[4,2,16,512]{3,2,1,0:T(8,128)(2,1)S(1)}, u32[]{:S(2)}, u32[]{:S(2)}) collective-permute-start(bf16[4,2,16,512]{3,2,1,0:T(8,128)(2,1)S(1)} %get-tuple-element.16), channel_id=1, source_target_pairs={{0,1},{1,0},{2,3},{3,2},{4,5},{5,4},{6,7},{7,6},{8,9},{9,8},{10,11... | collective-permute-start | bytes 393224 | tf_op jit(solution)/shard_map/ppermute | solution.py:520
  5.3 14.4 %slice-start = ((s8[8388608]{0:T(1024)(128)(4,1)}), s8[4194304]{0:T(1024)(128)(4,1)S(1)}, s32[]{:S(2)}) async-start(s8[8388608]{0:T(1024)(128)(4,1)} %bitcast.3), calls=%async_computation | async-start | bytes 8388608
  5.3 6.1 %collective-permute-start.4 = (s32[1,10]{1,0:T(1,128)S(1)}, s32[1,10]{1,0:T(1,128)S(1)}, u32[]{:S(2)}, u32[]{:S(2)}) collective-permute-start(s32[1,10]{1,0:T(1,128)S(1)} %lead.1.own_ref), channel_id=1, source_target_pairs={{0,16},{8,24},{16,0},{24,8},{1,17},{9,25},{17,1},{25,9},{2,18},{10... | collective-permute-start | bytes 128 | tf_op jit(solution)/shard_map/ppermute | solution.py:520
  7.8 3.6 %collective-permute-start.3 = (s32[1,10]{1,0:T(1,128)S(1)}, s32[1,10]{1,0:T(1,128)S(1)}, u32[]{:S(2)}, u32[]{:S(2)}) collective-permute-start(s32[1,10]{1,0:T(1,128)S(1)} %lead.1.own_ref), channel_id=1, source_target_pairs={{0,8},{1,25},{2,10},{3,27},{4,12},{5,29},{6,14},{7,31},{8,0},{9,17... | collective-permute-start | bytes 128 | tf_op jit(solution)/shard_map/ppermute | solution.py:532
  11.4 1.2 %collective-permute-start.5 = (s32[1,10]{1,0:T(1,128)S(1)}, s32[1,10]{1,0:T(1,128)S(1)}, u32[]{:S(2)}, u32[]{:S(2)}) collective-permute-start(s32[1,10]{1,0:T(1,128)S(1)} %collective-permute-done.3.first_ref), channel_id=1, source_target_pairs={{0,1},{1,0},{2,3},{3,2},{4,5},{5,4},{6,7},{7,6},{8,9},{9,8},{10,11... | collective-permute-start | bytes 128 | tf_op jit(solution)/shard_map/ppermute | solution.py:520
  12.6 7.0 %slice-start.1 = ((s8[8388608]{0:T(1024)(128)(4,1)}), s8[4194304]{0:T(1024)(128)(4,1)S(1)}, s32[]{:S(2)}) async-start(s8[8388608]{0:T(1024)(128)(4,1)} %bitcast.3), calls=%async_computation.1 | async-start | bytes 8388608
  12.6 4.3 %collective-permute-start.1 = (bf16[2,2,16,512]{3,2,1,0:T(8,128)(2,1)S(1)}, bf16[2,2,16,512]{3,2,1,0:T(8,128)(2,1)S(1)}, u32[]{:S(2)}, u32[]{:S(2)}) collective-permute-start(bf16[2,2,16,512]{3,2,1,0:T(8,128)(2,1)S(1)} %get-tuple-element.18), channel_id=1, source_target_pairs={{0,2},{1,3},{2,0},{3,1},{4,6},{5,7},{6,4},{7,5},{8,10},{9,11},{10,... | collective-permute-start | bytes 196616 | tf_op jit(solution)/shard_map/ppermute | solution.py:520
  17.0 4.9 %collective-permute-start.2 = (bf16[1,2,16,512]{3,2,1,0:T(8,128)(2,1)S(1)}, bf16[1,2,16,512]{3,2,1,0:T(8,128)(2,1)S(1)}, u32[]{:S(2)}, u32[]{:S(2)}) collective-permute-start(bf16[1,2,16,512]{3,2,1,0:T(8,128)(2,1)S(1)} %get-tuple-element.20), channel_id=1, source_target_pairs={{0,4},{1,5},{2,6},{3,7},{4,0},{5,1},{6,2},{7,3},{8,12},{9,13},{10,... | collective-permute-start | bytes 98312 | tf_op jit(solution)/shard_map/ppermute | solution.py:520
  22.1 4.3 %collective-permute-start.6 = (bf16[32,128]{1,0:T(8,128)(2,1)S(1)}, bf16[32,128]{1,0:T(8,128)(2,1)S(1)}, u32[]{:S(2)}, u32[]{:S(2)}) collective-permute-start(bf16[32,128]{1,0:T(8,128)(2,1)S(1)} %get-tuple-element.22), channel_id=1, source_target_pairs={{0,8},{8,0},{16,24},{24,16},{1,9},{9,1},{17,25},{25,17},{2,10},{10... | collective-permute-start | bytes 24584 | tf_op jit(solution)/shard_map/ppermute | solution.py:520
  23.7 3.7 %collective-permute-start.7 = (bf16[32,128]{1,0:T(8,128)(2,1)S(1)}, bf16[32,128]{1,0:T(8,128)(2,1)S(1)}, u32[]{:S(2)}, u32[]{:S(2)}) collective-permute-start(bf16[32,128]{1,0:T(8,128)(2,1)S(1)} %get-tuple-element.23), channel_id=1, source_target_pairs={{0,16},{8,24},{16,0},{24,8},{1,17},{9,25},{17,1},{25,9},{2,18},{10... | collective-permute-start | bytes 24584 | tf_op jit(solution)/shard_map/ppermute | solution.py:520
  24.2 4.5 %collective-permute-start.8 = (bf16[32,128]{1,0:T(8,128)(2,1)S(1)}, bf16[32,128]{1,0:T(8,128)(2,1)S(1)}, u32[]{:S(2)}, u32[]{:S(2)}) collective-permute-start(bf16[32,128]{1,0:T(8,128)(2,1)S(1)} %get-tuple-element.24), channel_id=1, source_target_pairs={{0,24},{8,16},{16,8},{24,0},{1,25},{9,17},{17,9},{25,1},{2,26},{10... | collective-permute-start | bytes 24584 | tf_op jit(solution)/shard_map/ppermute | solution.py:520
